TPU v7x, 32 devices: a whole 2x2x4 slice. The times are simulated.
32 devices in a mesh: pair: 2 (over x), tp: 4 (over z), side: 4 (over y, core).
Axes of the slice: x: 2, y: 2, z: 4, core: 2. Of those that a mesh axis runs over, the one named last changes fastest.
Arguments:
- x_prompt: bfloat16 [8, 512, 5120], P(('pair', 'side')), parts along dimension 0
- s_len: int32 [8], P(('pair', 'side')), parts along dimension 0
- y_tok: bfloat16 [8, 2, 5120], P(('pair', 'side')), parts along dimension 0
- k_cache: bfloat16 [8, 1, 2, 128, 128, 192], P(('pair', 'side'), None, None, None, 'tp'), parts along dimension 0
- v_cache: bfloat16 [8, 1, 2, 128, 128, 128], P(('pair', 'side'), None, None, None, 'tp'), parts along dimension 0
- c_len: int32 [8, 2], P(('pair', 'side')), parts along dimension 0
- attn_gain: bfloat16 [1, 5120], replicated
- w_q: bfloat16 [1, 5120, 128, 192], P(None, None, 'tp')
- w_dkv: bfloat16 [1, 5120, 576], replicated
- w_uk: bfloat16 [1, 512, 128, 128], P(None, None, 'tp')
- w_uv: bfloat16 [1, 512, 128, 128], P(None, None, 'tp')
- w_o: bfloat16 [1, 128, 128, 5120], P(None, 'tp')
- mlp_gain: bfloat16 [1, 5120], replicated
- w_gate: bfloat16 [1, 5120, 12288], P(None, None, 'tp')
- w_up: bfloat16 [1, 5120, 12288], P(None, None, 'tp')
- w_down: bfloat16 [1, 12288, 5120], P(None, 'tp')
Outputs:
- output 1: bfloat16 [8, 512, 5120], P(('pair', 'side')), parts along dimension 0
- output 2: bfloat16 [8, 2, 5120], P(('pair', 'side')), parts along dimension 0
- output 3: bfloat16 [8, 1, 512, 128, 192], P(('pair', 'side'), None, None, 'tp'), parts along dimension 0
- output 4: bfloat16 [8, 1, 512, 128, 128], P(('pair', 'side'), None, None, 'tp'), parts along dimension 0
- output 5: bfloat16 [8, 1, 2, 128, 128, 192], P(('pair', 'side'), None, None, None, 'tp'), parts along dimension 0
- output 6: bfloat16 [8, 1, 2, 128, 128, 128], P(('pair', 'side'), None, None, None, 'tp'), parts along dimension 0
There are 2 independent parts. A program takes and returns all parts, laid end to end along the dimension named above; an argument that names none is the same for every part.
All inputs are finite; a program needn't handle non-finite values.
Results may differ from a plain program's by a relative error of at most 0.0108281.
Values are sent between devices in bfloat16 or wider.
A program may use at most 1 GiB of HBM per device.

v0:
```python
import jax
import jax.numpy as jnp
from jax import lax
from jax.sharding import PartitionSpec as P

EPSILON = 1e-6
THETA = 10000.0


def rms_scaled(values, gain):
    hidden = values.astype(jnp.float32)
    inv_rms = lax.rsqrt(jnp.mean(hidden * hidden, axis=-1, keepdims=True) + EPSILON)
    return (hidden * inv_rms * gain.astype(jnp.float32)).astype(jnp.bfloat16)


def rms_plain(values):
    hidden = values.astype(jnp.float32)
    inv_rms = lax.rsqrt(jnp.mean(hidden * hidden, axis=-1, keepdims=True) + EPSILON)
    return (hidden * inv_rms).astype(jnp.bfloat16)


def apply_rope(values, positions):
    half_dim = values.shape[-1] // 2
    inv_freq = THETA ** (-jnp.arange(half_dim, dtype=jnp.float32) * 2.0 / values.shape[-1])
    angles = positions.astype(jnp.float32)[..., None] * inv_freq
    cos_part = jnp.cos(angles)
    sin_part = jnp.sin(angles)
    first_half = values[..., :half_dim].astype(jnp.float32)
    second_half = values[..., half_dim:].astype(jnp.float32)
    return jnp.concatenate([first_half * cos_part - second_half * sin_part, second_half * cos_part + first_half * sin_part], axis=-1).astype(jnp.bfloat16)


def make_query(normed, w_q_layer, positions, nope_dim):
    query_all = jnp.einsum('sd,dhe->she', normed, w_q_layer, preferred_element_type=jnp.float32).astype(jnp.bfloat16)
    return jnp.concatenate([query_all[..., :nope_dim], apply_rope(query_all[..., nope_dim:], positions[:, None])], axis=-1)


def make_latent(normed, w_dkv_layer, positions, rank_dim):
    latent_raw = jnp.dot(normed, w_dkv_layer, preferred_element_type=jnp.float32).astype(jnp.bfloat16)
    return jnp.concatenate([rms_plain(latent_raw[:, :rank_dim]), apply_rope(latent_raw[:, rank_dim:], positions)], axis=-1)


def expand_latent(latent_pack, w_uk_layer, w_uv_layer):
    rank_dim = w_uk_layer.shape[0]
    latent = latent_pack[:, :rank_dim]
    rope_key = latent_pack[:, rank_dim:]
    key_nope = jnp.einsum('sr,rhn->shn', latent, w_uk_layer, preferred_element_type=jnp.float32).astype(jnp.bfloat16)
    value_full = jnp.einsum('sr,rhv->shv', latent, w_uv_layer, preferred_element_type=jnp.float32).astype(jnp.bfloat16)
    rope_heads = jnp.broadcast_to(rope_key[:, None, :], (key_nope.shape[0], key_nope.shape[1], rope_key.shape[1]))
    return jnp.concatenate([key_nope, rope_heads], axis=-1), value_full


def masked_softmax(scores, allowed):
    return jax.nn.softmax(jnp.where(allowed, scores, -1e30), axis=-1).astype(jnp.bfloat16)


def prompt_attention(query_all, key_full, value_full, valid_len):
    seq_len = query_all.shape[0]
    scores = jnp.einsum('qhe,khe->hqk', query_all, key_full, preferred_element_type=jnp.float32) * query_all.shape[-1] ** -0.5
    row_pos = jnp.arange(seq_len)[:, None]
    col_pos = jnp.arange(seq_len)[None, :]
    allowed = (col_pos <= row_pos) & (col_pos < valid_len)
    probs_bf = masked_softmax(scores, allowed[None])
    return jnp.einsum('hqk,khv->qhv', probs_bf, value_full, preferred_element_type=jnp.float32).astype(jnp.bfloat16)


def cache_attention(query_all, key_layer, value_layer, cur_len):
    scores = jnp.einsum('bhe,bthe->bht', query_all, key_layer, preferred_element_type=jnp.float32) * query_all.shape[-1] ** -0.5
    allowed = jnp.arange(key_layer.shape[1])[None, None, :] <= cur_len[:, None, None]
    probs_bf = masked_softmax(scores, allowed)
    return jnp.einsum('bht,bthv->bhv', probs_bf, value_layer, preferred_element_type=jnp.float32).astype(jnp.bfloat16)


def head_merge(attn_val, w_o_layer):
    return jnp.einsum('shv,hvd->sd', attn_val, w_o_layer, preferred_element_type=jnp.float32)


def mlp_partial(normed, w_gate_layer, w_up_layer, w_down_layer):
    gate_val = jnp.dot(normed, w_gate_layer, preferred_element_type=jnp.float32)
    up_val = jnp.dot(normed, w_up_layer, preferred_element_type=jnp.float32)
    act_val = (jax.nn.silu(gate_val) * up_val).astype(jnp.bfloat16)
    return jnp.dot(act_val, w_down_layer, preferred_element_type=jnp.float32)


def prompt_layer(hidden, valid_len, layer_w, reduce_fn):
    gain_attn, w_q_l, w_dkv_l, w_uk_l, w_uv_l, w_o_l, gain_mlp, w_gate_l, w_up_l, w_down_l = layer_w
    positions = jnp.arange(hidden.shape[0])
    normed = rms_scaled(hidden, gain_attn)
    query_all = make_query(normed, w_q_l, positions, w_uk_l.shape[-1])
    latent_pack = make_latent(normed, w_dkv_l, positions, w_uk_l.shape[0])
    key_full, value_full = expand_latent(latent_pack, w_uk_l, w_uv_l)
    attn_val = prompt_attention(query_all, key_full, value_full, valid_len)
    hidden = hidden + reduce_fn(head_merge(attn_val, w_o_l)).astype(jnp.bfloat16)
    hidden = hidden + reduce_fn(mlp_partial(rms_scaled(hidden, gain_mlp), w_gate_l, w_up_l, w_down_l)).astype(jnp.bfloat16)
    return hidden, latent_pack, key_full, value_full


def token_layer(tok_state, cur_len, key_old, value_old, layer_w, reduce_fn):
    gain_attn, w_q_l, w_dkv_l, w_uk_l, w_uv_l, w_o_l, gain_mlp, w_gate_l, w_up_l, w_down_l = layer_w
    normed = rms_scaled(tok_state, gain_attn)
    query_all = make_query(normed, w_q_l, cur_len, w_uk_l.shape[-1])
    latent_pack = make_latent(normed, w_dkv_l, cur_len, w_uk_l.shape[0])
    key_new, value_new = expand_latent(latent_pack, w_uk_l, w_uv_l)
    slot_hit = (jnp.arange(key_old.shape[1])[None, :] == cur_len[:, None])[:, :, None, None]
    key_layer = jnp.where(slot_hit, key_new[:, None], key_old)
    value_layer = jnp.where(slot_hit, value_new[:, None], value_old)
    attn_val = cache_attention(query_all, key_layer, value_layer, cur_len)
    tok_state = tok_state + reduce_fn(head_merge(attn_val, w_o_l)).astype(jnp.bfloat16)
    tok_state = tok_state + reduce_fn(mlp_partial(rms_scaled(tok_state, gain_mlp), w_gate_l, w_up_l, w_down_l)).astype(jnp.bfloat16)
    return tok_state, key_layer, value_layer


def tp_sum(values):
    return lax.psum(values, 'tp')


def solution(mesh):
    groups = mesh.shape['side']
    shift_pairs = [(source_idx, (source_idx + 1) % groups) for source_idx in range(groups)]
    group_axes = ('pair', 'side')
    head_spec = P(None, None, 'tp', None)
    cache_spec = P(group_axes, None, None, None, 'tp', None)
    prompt_spec = P(group_axes, None, None, 'tp', None)
    row_spec = P(group_axes, None, None)
    spec_in = (row_spec, P(group_axes), row_spec, cache_spec, cache_spec, P(group_axes, None), P(), head_spec, P(), head_spec, head_spec, P(None, 'tp', None, None), P(), P(None, None, 'tp'), P(None, None, 'tp'), P(None, 'tp', None))
    spec_out = (row_spec, row_spec, prompt_spec, prompt_spec, cache_spec, cache_spec)

    def device_step(x_prompt, s_len, y_tok, k_cache, v_cache, c_len, attn_gain, w_q, w_dkv, w_uk, w_uv, w_o, mlp_gain, w_gate, w_up, w_down):
        weights = (attn_gain, w_q, w_dkv, w_uk, w_uv, w_o, mlp_gain, w_gate, w_up, w_down)
        hidden = x_prompt[0]
        tok_state = y_tok[0]
        key_recv = []
        value_recv = []
        key_next = []
        value_next = []
        for layer_idx in range(w_q.shape[0]):
            layer_w = tuple(stacked[layer_idx] for stacked in weights)
            hidden, latent_pack, key_full, value_full = prompt_layer(hidden, s_len[0], layer_w, tp_sum)
            received = lax.ppermute(latent_pack, 'side', shift_pairs)
            key_in, value_in = expand_latent(received, layer_w[3], layer_w[4])
            key_recv.append(key_in)
            value_recv.append(value_in)
            tok_state, key_layer, value_layer = token_layer(tok_state, c_len[0], k_cache[0, layer_idx], v_cache[0, layer_idx], layer_w, tp_sum)
            key_next.append(key_layer)
            value_next.append(value_layer)
        return (hidden[None], tok_state[None], jnp.stack(key_recv)[None], jnp.stack(value_recv)[None], jnp.stack(key_next)[None], jnp.stack(value_next)[None])

    return jax.shard_map(device_step, mesh=mesh, in_specs=spec_in, out_specs=spec_out, check_vma=False)
```

profile of v0, /device:TPU:0, one launch (start us, length us, event | category | flops | bytes accessed | tf_op | source)
XLA Modules:
  0.0 1084.8 jit_solution(2777807735175107599)
XLA Ops:
  0.7 0.8 mul.393
  1.4 0.0 slice-start.4
  1.4 3.7 multiply_reduce_fusion
  5.2 0.0 slice-start.5
  5.2 7.7 fusion.89
  12.9 0.2 fusion.105
  13.0 0.1 fusion.106
  13.2 0.3 fusion.114
  13.5 0.9 pad_maximum_fusion
  14.4 0.7 collective-permute-start
  15.1 0.2 multiply_reduce_fusion.1
  15.3 0.0 slice-start.2
  15.3 1.6 fusion.102
  16.9 25.1 %fusion.3 = bf16[2,32,192]{2,0,1:T(2,128)(2,1)} fusion(bf16[1,5120,32,192]{1,3,2,0:T(8,128)(2,1)} %param.23, bf16[1,2,5120]{2,1,0:T(2,128)(2,1)S(1)} %copy-done.9, f32[2]{0:T(128)S(1)} %add_rsqrt_fusion.5, f32[5120]{0:T(1024)S(1)} %bitcast.163), kind=kOutput, calls=%fused_computation.3 | convolution fusion | flops 125870080 | bytes 62980104 | tf_op jit(solution)/shard_map/sd,dhe->she/dot_general | solution.py:34
  42.0 39.8 %fusion.83 = f32[512,6144]{0,1} fusion(bf16[5120,6144]{0,1:T(8,128)(2,1)} %bitcast.143, bf16[1,512,5120]{2,1,0:T(8,128)(2,1)S(1)} %bitcast.149, f32[5120]{0:T(1024)S(1)} %bitcast.164, f32[512]{0:T(512)S(1)} %add_rsqrt_fusion.2), kind=kOutput, calls=%fused_computation.86 | convolution fusion | flops 32222740480 | bytes 80762880
  81.8 8.2 convert_element_type.207
  90.0 7.8 copy.47
  97.9 7.0 fusion.69
  104.8 0.1 fusion.136
  104.9 1.2 fusion.98
  106.2 1.2 convolution_convert_fusion
  107.3 2.4 fusion.161
  109.7 0.6 convert_element_type.211
  110.4 2.3 slice.69
  113.3 0.1 fusion.107
  113.5 2.0 fusion.77
  115.5 0.2 broadcast_in_dim.71
  115.7 14.8 %fusion.32 = f32[32,512,512]{1,2,0:T(8,128)} fusion(bf16[512,32,32]{0,2,1:T(8,128)(2,1)} %get-tuple-element.33, bf16[512,32,32]{0,2,1:T(8,128)(2,1)} %get-tuple-element.32, bf16[512,32,128]{0,2,1:T(8,128)(2,1)} %slice.69, bf16[512,32,64]{0,2,1:T(8,128)(2,1)S(1)} %broadcast_in_dim.71, bf16[512,32,128]{0,2,1:T(8,128)(2,1)S(1)} %convert_element_type.211), kind=kOutput, calls=%fused_computation.37 | convolution fusion | flops 3252682752 | bytes 46137344 | tf_op jit(solution)/shard_map/qhe,khe->hqk/dot_general | solution.py:59
  130.6 34.4 %fusion.160 = (f32[32,512]{1,0:T(8,128)S(1)}, f32[32,512,512]{1,2,0:T(8,128)}) fusion(f32[32,512,512]{1,2,0:T(8,128)} %fusion.32, pred[512,512]{0,1:T(8,128)(4,1)S(1)} %fusion.107), kind=kOutput, calls=%fused_computation.192 | output fusion | flops 50332160 | bytes 67436544 | tf_op jit(solution)/shard_map/sub | solution.py:54
  165.0 15.4 %fusion.182 = bf16[512,32,128]{0,2,1:T(8,128)(2,1)} fusion(f32[32,512,512]{1,2,0:T(8,128)} %get-tuple-element.47, f32[32,512]{1,0:T(8,128)S(1)} %get-tuple-element.46, bf16[512,32,128]{2,0,1:T(8,128)(2,1)} %fusion.69), kind=kOutput, calls=%fused_computation.56.clone.1 | convolution fusion | flops 2166358016 | bytes 42008576 | tf_op jit(solution)/shard_map/hqk,khv->qhv/dot_general | solution.py:64
  180.4 0.0 copy-start.7
  180.4 29.7 %fusion.29 = f32[512,5120]{1,0:T(8,128)} fusion(bf16[1,32,128,5120]{3,2,1,0:T(8,128)(2,1)} %param.27, bf16[512,32,128]{0,2,1:T(8,128)(2,1)} %fusion.182), kind=kOutput, calls=%fused_computation.36 | convolution fusion | flops 21474836480 | bytes 56623104 | tf_op jit(solution)/shard_map/shv,hvd->sd/dot_general | solution.py:75
  210.1 0.1 fusion.141
  210.3 0.1 pad_maximum_fusion.3
  210.4 0.1 iota_compare_fusion.3
  210.5 0.0 copy-start.11
  210.5 0.1 fusion.122
  210.6 0.1 maximum_bitcast_fusion.1
  210.7 2.4 fusion.71
  213.1 0.2 fusion.101
  213.3 0.5 bitcast_select_fusion.2
  213.7 0.8 fusion.80
  214.6 14.8 %fusion.45 = f32[2,5120]{1,0:T(2,128)S(1)} fusion(bf16[1,32,128,5120]{3,2,1,0:T(8,128)(2,1)} %param.27, bf16[2,32,1,128]{3,2,1,0:T(2,128)(2,1)S(1)} %fusion.80), kind=kOutput, calls=%fused_computation.52 | convolution fusion | flops 83886080 | bytes 42000384 | tf_op jit(solution)/shard_map/shv,hvd->sd/dot_general | solution.py:75
  229.4 359.3 %all-reduce.4 = (bf16[512,5120]{1,0:T(8,128)(2,1)}, bf16[2,5120]{1,0:T(2,128)(2,1)S(1)}) all-reduce(f32[512,5120]{1,0:T(8,128)} %fusion.29, f32[2,5120]{1,0:T(2,128)S(1)} %fusion.45), channel_id=1, replica_groups=mesh['pair'=2,'tp'=4,'side'=4] {'tp'}, use_global_device_ids=true, to_apply=%region_4.5 | all-reduce | flops 2631680 | bytes 15790080 | tf_op jit(solution)/shard_map/psum | solution.py:114
  588.7 0.2 fusion.118
  588.9 12.1 %fusion.17 = f32[2,3072]{1,0:T(2,128)S(1)} fusion(bf16[1,5120,3072]{2,1,0:T(8,128)(2,1)} %param.29, bf16[2,5120]{1,0:T(2,128)(2,1)S(1)} %get-tuple-element.29, f32[2]{0:T(128)S(1)} %add_rsqrt_fusion.3, f32[5120]{0:T(1024)S(1)} %bitcast.157), kind=kOutput, calls=%fused_computation.20 | convolution fusion | flops 62955520 | bytes 31522824 | tf_op jit(solution)/shard_map/dot_general | solution.py:79
  601.0 22.1 %fusion.9 = f32[2,5120]{1,0:T(2,128)S(1)} fusion(bf16[1,3072,5120]{2,1,0:T(8,128)(2,1)} %param.31, bf16[1,5120,3072]{2,1,0:T(8,128)(2,1)} %param.30, f32[2,3072]{1,0:T(2,128)S(1)} %fusion.17, bf16[2,5120]{1,0:T(2,128)(2,1)S(1)} %get-tuple-element.29, f32[2]{0:T(128)S(1)} %add_rsqrt_fusion.3, f32[5120]{0:T(1024)S(1)} %bitcast.158), kind=kOutput, calls=%fused_computation.12 | convolution fusion | flops 125906944 | bytes 63021064 | tf_op jit(solution)/shard_map/dot_general | solution.py:82
  623.1 6.5 fusion.26
  629.6 24.0 %fusion.19 = f32[512,3072]{1,0:T(8,128)} fusion(bf16[1,5120,3072]{2,1,0:T(8,128)(2,1)} %param.29, bf16[512,5120]{1,0:T(8,128)(2,1)S(1)} %get-tuple-element.31, f32[5120]{0:T(1024)S(1)} %bitcast.159, f32[512]{0:T(512)S(1)} %add_rsqrt_fusion), kind=kOutput, calls=%fused_computation.22 | convolution fusion | flops 16116613120 | bytes 43014144 | tf_op jit(solution)/shard_map/dot_general | solution.py:79
  653.6 21.9 %multiply_convert_fusion.1.clone.4 = bf16[512,3072]{1,0:T(8,128)(2,1)S(1)} fusion(f32[512,3072]{1,0:T(8,128)} %fusion.19, bf16[1,5120,3072]{2,1,0:T(8,128)(2,1)} %param.30, bf16[512,5120]{1,0:T(8,128)(2,1)S(1)} %get-tuple-element.31, f32[5120]{0:T(1024)S(1)} %bitcast.160, f32[512]{0:T(512)S(1)} %add_rsqrt_fusion), kind=kOutput, calls=%fused_computation.47.clone.clone.clone.1 | convolution fusion | flops 16126050304 | bytes 46159872 | tf_op jit(solution)/shard_map/dot_general | solution.py:80
  675.5 24.4 %fusion.11 = f32[512,5120]{1,0:T(8,128)} fusion(bf16[1,3072,5120]{2,1,0:T(8,128)(2,1)} %param.31, bf16[512,3072]{1,0:T(8,128)(2,1)S(1)} %multiply_convert_fusion.1.clone.4), kind=kOutput, calls=%fused_computation.14 | convolution fusion | flops 16106127360 | bytes 45088768 | tf_op jit(solution)/shard_map/dot_general | solution.py:82
  699.9 353.5 %all-reduce.5 = (bf16[512,5120]{1,0:T(8,128)(2,1)}, bf16[2,5120]{1,0:T(2,128)(2,1)S(1)}) all-reduce(f32[512,5120]{1,0:T(8,128)} %fusion.11, f32[2,5120]{1,0:T(2,128)S(1)} %fusion.9), channel_id=1, replica_groups=mesh['pair'=2,'tp'=4,'side'=4] {'tp'}, use_global_device_ids=true, to_apply=%region_6.7 | all-reduce | flops 2631680 | bytes 15790080 | tf_op jit(solution)/shard_map/psum | solution.py:114
  1053.4 0.6 add_bitcast_fusion.1
  1054.1 7.1 add_bitcast_fusion
  1061.2 1.5 broadcast_select_fusion.1
  1062.7 3.2 broadcast_select_fusion
  1065.9 3.4 fusion.111
  1069.3 0.6 convert_element_type.244
  1070.0 1.5 copy-done.6
  1071.5 3.9 convert_bitcast_fusion
  1075.4 4.7 copy.62
  1080.2 0.8 slice.81
  1081.0 0.2 broadcast_in_dim.131
  1081.2 3.1 maximum_bitcast_fusion
  (72 shorter events, 0.3 us)
Async XLA Ops:
  0.6 12.5 %copy-start.19 = (f32[32]{0:T(128)}, f32[32]{0:T(128)S(1)}, u32[]{:S(2)}) copy-start(f32[32]{0:T(128)S(1)} %multiply_power_fusion) | copy-start | bytes 388
  1.4 13.8 %slice-start.4 = ((s8[5898240]{0:T(1024)(128)(4,1)}), s8[4194304]{0:T(1024)(128)(4,1)S(1)}, s32[]{:S(2)}) async-start(s8[5898240]{0:T(1024)(128)(4,1)} %bitcast.151), calls=%async_computation.4 | async-start | bytes 8388608
  5.2 9.9 copy-start.9
  5.2 10.1 slice-start.5
  14.4 1051.6 %collective-permute-start = (bf16[512,576]{0,1:T(8,128)(2,1)}, bf16[512,576]{0,1:T(8,128)(2,1)}, u32[]{:S(2)}, u32[]{:S(2)}) collective-permute-start(bf16[512,576]{0,1:T(8,128)(2,1)} %pad_maximum_fusion), channel_id=1, source_target_pairs={{0,1},{1,2},{2,3},{3,0},{4,5},{5,6},{6,7},{7,4},{8,9},{9,10},{10,1... | collective-permute-start | bytes 1769480 | tf_op jit(solution)/shard_map/ppermute | solution.py:139
  15.3 26.7 %slice-start.2 = ((s8[5242880]{0:T(1024)(128)(4,1)}), s8[4194304]{0:T(1024)(128)(4,1)S(1)}, s32[]{:S(2)}) async-start(s8[5242880]{0:T(1024)(128)(4,1)} %bitcast.148), calls=%async_computation.2 | async-start | bytes 8388608
  16.9 25.1 %slice-start.3 = ((s8[5242880]{0:T(1024)(128)(4,1)}), s8[1048576]{0:T(1024)(128)(4,1)S(1)}, s32[]{:S(2)}) async-start(s8[5242880]{0:T(1024)(128)(4,1)} %bitcast.148), calls=%async_computation.3 | async-start | bytes 2097152
  97.8 7.1 copy-start.5
  97.8 8.3 copy-start
  106.2 4.2 slice-start
  107.3 3.0 slice-start.1
  180.4 29.7 %copy-start.21 = (s32[1,2]{1,0:T(1,128)S(1)}, s32[1,2]{1,0:T(1,128)}, u32[]{:S(2)}) copy-start(s32[1,2]{1,0:T(1,128)} %param.21) | copy-start | bytes 28
  180.4 29.7 %copy-start.20 = (f32[32]{0:T(128)S(1)}, f32[32]{0:T(128)}, u32[]{:S(2)}) copy-start(f32[32]{0:T(128)} %copy-done.19) | copy-start | bytes 388
  180.4 29.8 %copy-start.15 = (bf16[2,32,192]{2,0,1:T(2,128)(2,1)S(1)}, bf16[2,32,192]{2,0,1:T(2,128)(2,1)}, u32[]{:S(2)}) copy-start(bf16[2,32,192]{2,0,1:T(2,128)(2,1)} %fusion.3) | copy-start | bytes 73732
  180.4 30.3 %copy-start.7 = (bf16[1,1,2,128,32,192]{3,5,4,2,1,0:T(8,128)(2,1)S(1)}, bf16[1,1,2,128,32,192]{3,5,4,2,1,0:T(8,128)(2,1)}, u32[]{:S(2)}) copy-start(bf16[1,1,2,128,32,192]{3,5,4,2,1,0:T(8,128)(2,1)} %param.19) | copy-start | bytes 9437188
  210.1 3.2 copy-start.3
  210.4 2.7 copy-start.13
  210.5 4.1 copy-start.17
  210.5 4.0 copy-start.11
  229.4 359.3 %copy-start.10 = (bf16[1,2,5120]{2,1,0:T(2,128)(2,1)S(1)}, bf16[1,2,5120]{2,1,0:T(2,128)(2,1)}, u32[]{:S(2)}) copy-start(bf16[1,2,5120]{2,1,0:T(2,128)(2,1)} %param.18) | copy-start | bytes 61444
  229.4 359.5 %copy-start.16 = (bf16[1,5120]{1,0:T(2,128)(2,1)S(1)}, bf16[1,5120]{1,0:T(2,128)(2,1)}, u32[]{:S(2)}) copy-start(bf16[1,5120]{1,0:T(2,128)(2,1)} %param.28) | copy-start | bytes 30724
  629.6 24.0 %copy-start.2 = (bf16[512,5120]{1,0:T(8,128)(2,1)}, bf16[512,5120]{1,0:T(8,128)(2,1)S(1)}, u32[]{:S(2)}) copy-start(bf16[512,5120]{1,0:T(8,128)(2,1)S(1)} %get-tuple-element.31) | copy-start | bytes 15728644
  1054.1 7.1 copy-start.4
  1054.1 7.1 copy-start.12
  1054.1 7.1 copy-start.18
  1054.1 8.7 copy-start.8
  1054.1 8.7 copy-start.14
  1061.2 4.8 copy-start.1
  1069.3 2.2 copy-start.6
where the time goes:
time: 1090 us; the launch traced here: 1080 us
  blocking collectives  713 us (65%)
  matrix products  276 us (25%)
  other arithmetic  75.7 us (7%)
  local copies, waits for them, and re-layouts  17.8 us (2%)
    psum x2, blocking collectives, tp_sum(): return lax.psum(values, 'tp')  713 us
    dot_general x2, matrix products, mlp_partial(): return jnp.dot(act_val, w_down_layer, preferred_element_type=jnp.float32)  46.5 us
    unnamed x3, matrix products  45.6 us
    dot_general x2, matrix products, head_merge(): jnp.einsum('shv,hvd->sd', attn_val, w_o_layer, preferred_element_type=jnp...  44.5 us
    dot_general x2, matrix products, mlp_partial(): gate_val = jnp.dot(normed, w_gate_layer, preferred_element_type=jnp.float32)  36.1 us
    sub x1, other arithmetic, masked_softmax(): jax.nn.softmax(jnp.where(allowed, scores, -1e+30), axis=-1)  34.4 us
    dot_general x1, matrix products, make_query(): jnp.einsum('sd,dhe->she', normed, w_q_layer, preferred_element_type=jnp.f...  25.1 us
    dot_general x1, matrix products, mlp_partial(): up_val = jnp.dot(normed, w_up_layer, preferred_element_type=jnp.float32)  21.9 us
  transfers between devices with their start and end apart: 1, of which 0 were waited for; matrix products, arithmetic and copies ran while one was open for 31% of the time, Pallas kernels for 0%

commit v1 on v0

v1 whole, which is shorter than its diff:
```python
import functools

import jax
import jax.numpy as jnp
from jax import lax
from jax.experimental import pallas as pl
from jax.experimental.pallas import tpu as pltpu
from jax.sharding import PartitionSpec as P

EPSILON = 1e-6
THETA = 10000.0

SUB = 128
CHUNK = 2 * SUB
LAG = 2
RING_OWN = 16
RING_LAND = 32
RING_SEND = 16
DEC = 8
MESH = pl.DeviceIdType.MESH


def rms_scaled(values, gain):
    hidden = values.astype(jnp.float32)
    inv_rms = lax.rsqrt(jnp.mean(hidden * hidden, axis=-1, keepdims=True) + EPSILON)
    return (hidden * inv_rms * gain.astype(jnp.float32)).astype(jnp.bfloat16)


def rms_plain(values):
    hidden = values.astype(jnp.float32)
    inv_rms = lax.rsqrt(jnp.mean(hidden * hidden, axis=-1, keepdims=True) + EPSILON)
    return (hidden * inv_rms).astype(jnp.bfloat16)


def apply_rope(values, positions):
    half_dim = values.shape[-1] // 2
    inv_freq = THETA ** (-jnp.arange(half_dim, dtype=jnp.float32) * 2.0 / values.shape[-1])
    angles = positions.astype(jnp.float32)[..., None] * inv_freq
    cos_part = jnp.cos(angles)
    sin_part = jnp.sin(angles)
    first_half = values[..., :half_dim].astype(jnp.float32)
    second_half = values[..., half_dim:].astype(jnp.float32)
    return jnp.concatenate([first_half * cos_part - second_half * sin_part, second_half * cos_part + first_half * sin_part], axis=-1).astype(jnp.bfloat16)


def make_query(normed, w_q_layer, positions, nope_dim):
    query_all = jnp.einsum('sd,dhe->she', normed, w_q_layer, preferred_element_type=jnp.float32).astype(jnp.bfloat16)
    return jnp.concatenate([query_all[..., :nope_dim], apply_rope(query_all[..., nope_dim:], positions[:, None])], axis=-1)


def make_latent(normed, w_dkv_layer, positions, rank_dim):
    latent_raw = jnp.dot(normed, w_dkv_layer, preferred_element_type=jnp.float32).astype(jnp.bfloat16)
    return jnp.concatenate([rms_plain(latent_raw[:, :rank_dim]), apply_rope(latent_raw[:, rank_dim:], positions)], axis=-1)


def expand_latent(latent_pack, w_uk_layer, w_uv_layer):
    rank_dim = w_uk_layer.shape[0]
    latent = latent_pack[:, :rank_dim]
    rope_key = latent_pack[:, rank_dim:]
    key_nope = jnp.einsum('sr,rhn->shn', latent, w_uk_layer, preferred_element_type=jnp.float32).astype(jnp.bfloat16)
    value_full = jnp.einsum('sr,rhv->shv', latent, w_uv_layer, preferred_element_type=jnp.float32).astype(jnp.bfloat16)
    rope_heads = jnp.broadcast_to(rope_key[:, None, :], (key_nope.shape[0], key_nope.shape[1], rope_key.shape[1]))
    return jnp.concatenate([key_nope, rope_heads], axis=-1), value_full


def masked_softmax(scores, allowed):
    return jax.nn.softmax(jnp.where(allowed, scores, -1e30), axis=-1).astype(jnp.bfloat16)


def prompt_attention(query_all, key_full, value_full, valid_len):
    seq_len = query_all.shape[0]
    scores = jnp.einsum('qhe,khe->hqk', query_all, key_full, preferred_element_type=jnp.float32) * query_all.shape[-1] ** -0.5
    row_pos = jnp.arange(seq_len)[:, None]
    col_pos = jnp.arange(seq_len)[None, :]
    allowed = (col_pos <= row_pos) & (col_pos < valid_len)
    probs_bf = masked_softmax(scores, allowed[None])
    return jnp.einsum('hqk,khv->qhv', probs_bf, value_full, preferred_element_type=jnp.float32).astype(jnp.bfloat16)


def cache_attention(query_all, key_layer, value_layer, cur_len):
    scores = jnp.einsum('bhe,bthe->bht', query_all, key_layer, preferred_element_type=jnp.float32) * query_all.shape[-1] ** -0.5
    allowed = jnp.arange(key_layer.shape[1])[None, None, :] <= cur_len[:, None, None]
    probs_bf = masked_softmax(scores, allowed)
    return jnp.einsum('bht,bthv->bhv', probs_bf, value_layer, preferred_element_type=jnp.float32).astype(jnp.bfloat16)


def block_kernel(n_tp, ap_ref, ad_ref, gain_ref, x_hbm, ys_hbm, wo_hbm, wg_hbm, wu_hbm, wd_hbm, out_hbm, outd_hbm,
                 hb, own, land, dec, wa, wb, b_buf, act, stat,
                 wa_sem, wb_sem, x_sem, out_sem, outd_sem, rs_send, rs_recv, ag_send, ag_recv):
    last = n_tp - 1
    hv = wo_hbm.shape[0]
    dm = wo_hbm.shape[1]
    ffn = wg_hbm.shape[1]
    half = dm // 2
    nt = half // SUB
    nf = ffn // SUB
    units = 2 * (2 * nt + 1)
    total = 2 * units
    z = lax.axis_index('tp')

    barrier = pltpu.get_barrier_semaphore()

    @pl.when(z > 0)
    def _():
        pl.semaphore_signal(barrier, inc=1, device_id={'tp': z - 1}, device_id_type=MESH)

    @pl.when(z < last)
    def _():
        pl.semaphore_signal(barrier, inc=1, device_id={'tp': z + 1}, device_id_type=MESH)

    pos = (z, last - z)
    nxt = (z + 1, z - 1)
    prv = (z - 1, z + 1)

    def wo_copies(q):
        slot = q % 3
        j = q % nt
        return [pltpu.make_async_copy(wo_hbm.at[:, pl.ds(pl.multiple_of(d * half + j * SUB, SUB), SUB)],
                                      wa.at[slot, pl.ds(0, hv), pl.ds(d * SUB, SUB)], wa_sem.at[slot]) for d in (0, 1)]

    def wd_copies(q):
        slot = q % 3
        j = q % nt
        return [pltpu.make_async_copy(wd_hbm.at[:, pl.ds(pl.multiple_of(d * half + j * SUB, SUB), SUB)],
                                      wa.at[slot, pl.ds(0, ffn), pl.ds(d * SUB, SUB)], wa_sem.at[slot]) for d in (0, 1)]

    def start_a(q):
        @pl.when(q < 2 * nt)
        def _():
            for copy in wo_copies(q):
                copy.start()

        @pl.when((q >= 2 * nt) & (q < 4 * nt))
        def _():
            for copy in wd_copies(q):
                copy.start()

    def start_b(q):
        @pl.when(q < 2 * nf)
        def _():
            slot = q % 3
            j = q % nf
            cols = pl.ds(pl.multiple_of(j * SUB, SUB), SUB)
            pltpu.make_async_copy(wg_hbm.at[:, cols], wb.at[slot, :, pl.ds(0, SUB)], wb_sem.at[slot]).start()
            pltpu.make_async_copy(wu_hbm.at[:, cols], wb.at[slot, :, pl.ds(SUB, SUB)], wb_sem.at[slot]).start()

    start_a(0)
    start_a(1)
    start_b(0)
    start_b(1)

    def x_copy(d, w):
        i = w // 2
        rows = pl.ds(pl.multiple_of((i // nt) * CHUNK + (w % 2) * SUB, SUB), SUB)
        cols = pl.ds(pl.multiple_of(d * half + (i % nt) * SUB, SUB), SUB)
        return rows, cols

    for d in (0, 1):
        @pl.when(pos[d] == last)
        def _():
            @pl.loop(0, 4 * nt)
            def _(w):
                rows, cols = x_copy(d, w)
                pltpu.make_async_copy(x_hbm.at[rows, cols], hb.at[d, w], x_sem).start()
            for s in (0, 1):
                pltpu.make_async_copy(ys_hbm.at[d, s], hb.at[d, 4 * nt + s], x_sem).start()

    dec[...] = jnp.zeros_like(dec)

    pl.semaphore_wait(barrier, jnp.where(z > 0, 1, 0) + jnp.where(z < last, 1, 0))

    for d in (0, 1):
        @pl.when(pos[d] == last)
        def _():
            pltpu.make_async_copy(hb.at[d, pl.ds(0, units)], hb.at[d, pl.ds(0, units)], x_sem).wait()

    def rs_copy(d, u):
        return pltpu.make_async_remote_copy(
            src_ref=own.at[d, u % RING_OWN], dst_ref=land.at[d, u % RING_LAND],
            send_sem=rs_send.at[d, u % RING_OWN], recv_sem=rs_recv.at[d, u % RING_LAND],
            device_id={'tp': nxt[d]}, device_id_type=MESH)

    def ag_copy(d, u):
        return pltpu.make_async_remote_copy(
            src_ref=hb.at[d, u], dst_ref=hb.at[d, u],
            send_sem=ag_send.at[d, u % RING_SEND], recv_sem=ag_recv.at[d, u % RING_LAND],
            device_id={'tp': prv[d]}, device_id_type=MESH)

    def give_back(d, u):
        @pl.when(u >= RING_SEND)
        def _():
            ag_copy(d, u).wait_send()
        ag_copy(d, u).start()

    def write_out(d, u):
        w = u - units

        @pl.when((w >= 0) & (w < 4 * nt))
        def _():
            rows, cols = x_copy(d, w)
            pltpu.make_async_copy(hb.at[d, u], out_hbm.at[rows, cols], out_sem).start()

        @pl.when(w >= 4 * nt)
        def _():
            pltpu.make_async_copy(hb.at[d, u], outd_hbm.at[d, w - 4 * nt], outd_sem).start()

    def tick(t):
        for d in (0, 1):
            p = pos[d]
            u = t - LAG * p

            @pl.when((u >= 0) & (u < total))
            def _():
                @pl.when(p == 0)
                def _():
                    rs_copy(d, u).start()

                @pl.when((p > 0) & (p < last))
                def _():
                    rs_copy(d, u).wait_recv()
                    own[d, u % RING_OWN] = own[d, u % RING_OWN] + land[d, u % RING_LAND]
                    rs_copy(d, u).start()

                @pl.when(p == last)
                def _():
                    rs_copy(d, u).wait_recv()
                    summed = (own[d, u % RING_OWN] + land[d, u % RING_LAND]).astype(jnp.bfloat16)
                    hb[d, u] = (hb[d, u % units].astype(jnp.float32) + summed.astype(jnp.float32)).astype(jnp.bfloat16)
                    give_back(d, u)
                    write_out(d, u)

        for d in (0, 1):
            p = pos[d]
            v = t - LAG * (2 * last - p)

            @pl.when((p < last) & (v >= 0) & (v < total))
            def _():
                ag_copy(d, v).wait_recv()

                @pl.when(p > 0)
                def _():
                    give_back(d, v)
                write_out(d, v)

    def free_own(i):
        for d in (0, 1):
            for s in (0, 1):
                u = 2 * i + s

                @pl.when((u >= RING_OWN) & (pos[d] < last))
                def _():
                    rs_copy(d, u).wait_send()

    def store_own(i, q, res, has_dec):
        free_own(i)
        for d in (0, 1):
            for s in (0, 1):
                own[d, (2 * i + s) % RING_OWN] = res[s * SUB:(s + 1) * SUB, d * SUB:(d + 1) * SUB]
            if has_dec:
                j = q % nt
                dec[d, pl.ds(pl.multiple_of(j * DEC, DEC), DEC), :] = res[CHUNK:CHUNK + DEC, d * SUB:(d + 1) * SUB]

    def wo_step(i, q, chunk):
        start_a(q + 2)
        slot = q % 3
        pltpu.make_async_copy(wa.at[slot, pl.ds(0, hv)], wa.at[slot, pl.ds(0, hv)], wa_sem.at[slot]).wait()
        if chunk == 0:
            lhs = ap_ref[0:CHUNK, :]
        else:
            lhs = jnp.concatenate([ap_ref[CHUNK:2 * CHUNK, :], ad_ref[...]], axis=0)
        res = jnp.dot(lhs, wa[slot, 0:hv, :], preferred_element_type=jnp.float32)
        store_own(i, q, res, chunk == 1)

    def down_step(i, q, chunk):
        start_a(q + 2)
        slot = q % 3
        pltpu.make_async_copy(wa.at[slot, pl.ds(0, ffn)], wa.at[slot, pl.ds(0, ffn)], wa_sem.at[slot]).wait()
        lhs = act[chunk, 0:CHUNK, :] if chunk == 0 else act[chunk]
        res = jnp.dot(lhs, wa[slot, 0:ffn, :], preferred_element_type=jnp.float32)
        store_own(i, q, res, chunk == 1)

    def gu_step(q, chunk):
        start_b(q + 2)
        slot = q % 3
        pltpu.make_async_copy(wb.at[slot], wb.at[slot], wb_sem.at[slot]).wait()
        rows = CHUNK if chunk == 0 else CHUNK + 2 * DEC
        res = jnp.dot(b_buf[0:rows, :], wb[slot], preferred_element_type=jnp.float32)
        j = q % nf
        value = (jax.nn.silu(res[:, :SUB]) * res[:, SUB:]).astype(jnp.bfloat16)
        act[chunk, 0:rows, pl.ds(pl.multiple_of(j * SUB, SUB), SUB)] = value

    def norm_chunk(chunk):
        for s in (0, 1):
            stat[...] = jnp.zeros_like(stat)

            @pl.loop(0, nt)
            def _(j):
                for d in (0, 1):
                    hid = hb[d, 2 * (chunk * nt + j) + s].astype(jnp.float32)
                    stat[...] = stat[...] + hid * hid
            inv = lax.rsqrt(jnp.sum(stat[...], axis=-1, keepdims=True) * (1.0 / dm) + EPSILON)
            stat[...] = jnp.broadcast_to(inv, stat.shape)

            @pl.loop(0, nt)
            def _(j):
                for d in (0, 1):
                    cols = pl.ds(pl.multiple_of(d * half + j * SUB, SUB), SUB)
                    hid = hb[d, 2 * (chunk * nt + j) + s].astype(jnp.float32)
                    b_buf[s * SUB:(s + 1) * SUB, cols] = (hid * stat[...] * gain_ref[:, cols].astype(jnp.float32)).astype(jnp.bfloat16)

    def norm_dec():
        per = SUB // DEC
        tiles = []
        for d in (0, 1):
            both = [hb[d, 4 * nt + s].astype(jnp.float32) for s in (0, 1)]
            for j in range(nt):
                r = (j % per) * DEC
                tiles.append(both[j // per][r:r + DEC, :])
        square = tiles[0] * tiles[0]
        for tile in tiles[1:]:
            square = square + tile * tile
        inv = lax.rsqrt(jnp.sum(square, axis=-1, keepdims=True) * (1.0 / dm) + EPSILON)
        pad = jnp.zeros((DEC, SUB), jnp.float32)
        for k, tile in enumerate(tiles):
            value = tile * inv * gain_ref[:, k * SUB:(k + 1) * SUB].astype(jnp.float32)
            b_buf[CHUNK:CHUNK + 2 * DEC, k * SUB:(k + 1) * SUB] = jnp.concatenate([value, pad], axis=0).astype(jnp.bfloat16)

    def dec_unit(i):
        free_own(i)
        for d in (0, 1):
            for s in (0, 1):
                own[d, (2 * i + s) % RING_OWN] = dec[d, s * SUB:(s + 1) * SUB, :]

    wait_units = (2 * nt - 1 + 2 * last * LAG) // 2 + 1
    wait_all = (4 * nt + 1 + 2 * last * LAG) // 2 + 1

    @pl.loop(0, nt)
    def _(i):
        wo_step(i, i, 0)
        tick(2 * i)
        tick(2 * i + 1)

    @pl.loop(nt, wait_units)
    def _(i):
        wo_step(i, i, 1)
        tick(2 * i)
        tick(2 * i + 1)

    norm_chunk(0)
    mid0 = wait_units + nf // 2

    @pl.loop(wait_units, mid0)
    def _(i):
        wo_step(i, i, 1)
        tick(2 * i)
        gu_step(2 * (i - wait_units), 0)
        tick(2 * i + 1)
        gu_step(2 * (i - wait_units) + 1, 0)

    @pl.loop(mid0, 2 * nt)
    def _(i):
        wo_step(i, i, 1)
        tick(2 * i)
        tick(2 * i + 1)

    dec_unit(2 * nt)
    tick(4 * nt)
    tick(4 * nt + 1)

    first = 2 * nt + 1

    @pl.loop(first, wait_all)
    def _(i):
        down_step(i, i - 1, 0)
        tick(2 * i)
        tick(2 * i + 1)

    norm_chunk(1)
    norm_dec()
    mid1 = wait_all + nf // 2

    @pl.loop(wait_all, mid1)
    def _(i):
        down_step(i, i - 1, 0)
        tick(2 * i)
        gu_step(nf + 2 * (i - wait_all), 1)
        tick(2 * i + 1)
        gu_step(nf + 2 * (i - wait_all) + 1, 1)

    @pl.loop(mid1, first + nt)
    def _(i):
        down_step(i, i - 1, 0)
        tick(2 * i)
        tick(2 * i + 1)

    @pl.loop(first + nt, first + 2 * nt)
    def _(i):
        down_step(i, i - 1, 1)
        tick(2 * i)
        tick(2 * i + 1)

    dec_unit(first + 2 * nt)

    @pl.loop(total - 2, total + 2 * last * LAG)
    def _(t):
        tick(t)

    for d in (0, 1):
        @pl.when(pos[d] < last)
        def _():
            @pl.loop(total - RING_OWN, total)
            def _(u):
                rs_copy(d, u).wait_send()

        @pl.when(pos[d] > 0)
        def _():
            @pl.loop(total - RING_SEND, total)
            def _(u):
                ag_copy(d, u).wait_send()

    pltpu.make_async_copy(hb.at[:, pl.ds(units, 4 * nt)], hb.at[:, pl.ds(units, 4 * nt)], out_sem).wait()
    pltpu.make_async_copy(hb.at[:, pl.ds(0, 2)], hb.at[:, pl.ds(0, 2)], outd_sem).wait()


def finish_block(n_tp, attn_prompt, attn_tok, mlp_gain, x_rows, y_stack, w_o, w_gate, w_up, w_down):
    dm = x_rows.shape[1]
    hv = w_o.shape[0]
    ffn = w_gate.shape[1]
    nt = dm // 2 // SUB
    units = 2 * (2 * nt + 1)
    bf, f32 = jnp.bfloat16, jnp.float32
    vmem = pl.BlockSpec(memory_space=pltpu.VMEM)
    hbm = pl.BlockSpec(memory_space=pl.ANY)
    sem = pltpu.SemaphoreType.DMA
    return pl.pallas_call(
        functools.partial(block_kernel, n_tp),
        out_shape=(jax.ShapeDtypeStruct(x_rows.shape, bf), jax.ShapeDtypeStruct((2, 2, SUB, SUB), bf)),
        in_specs=[vmem, vmem, vmem, hbm, hbm, hbm, hbm, hbm, hbm],
        out_specs=(hbm, hbm),
        scratch_shapes=[
            pltpu.VMEM((2, 2 * units, SUB, SUB), bf),
            pltpu.VMEM((2, RING_OWN, SUB, SUB), f32),
            pltpu.VMEM((2, RING_LAND, SUB, SUB), f32),
            pltpu.VMEM((2, CHUNK, SUB), f32),
            pltpu.VMEM((3, max(hv, ffn), 2 * SUB), bf),
            pltpu.VMEM((3, dm, 2 * SUB), bf),
            pltpu.VMEM((CHUNK + 2 * DEC, dm), bf),
            pltpu.VMEM((2, CHUNK + 2 * DEC, ffn), bf),
            pltpu.VMEM((SUB, SUB), f32),
            sem((3,)), sem((3,)), sem, sem, sem,
            sem((2, RING_OWN)), sem((2, RING_LAND)), sem((2, RING_SEND)), sem((2, RING_LAND)),
        ],
        compiler_params=pltpu.CompilerParams(collective_id=0, has_side_effects=True, vmem_limit_bytes=64000 * 1024),
    )(attn_prompt, attn_tok, mlp_gain, x_rows, y_stack, w_o, w_gate, w_up, w_down)


def stack_tokens(rows):
    nb, dm = rows.shape
    nt = dm // 2 // SUB
    tiles = jnp.transpose(rows.reshape(nb, 2, nt, SUB), (1, 2, 0, 3))
    tiles = jnp.pad(tiles, ((0, 0), (0, CHUNK // DEC - nt), (0, DEC - nb), (0, 0)))
    return tiles.reshape(2, 2, SUB, SUB)


def unstack_tokens(stack, nb, dm):
    nt = dm // 2 // SUB
    tiles = stack.reshape(2, CHUNK // DEC, DEC, SUB)[:, :nt, :nb]
    return jnp.transpose(tiles, (2, 0, 1, 3)).reshape(nb, dm)


def solution(mesh):
    groups = mesh.shape['side']
    n_tp = mesh.shape['tp']
    shift_pairs = [(source_idx, (source_idx + 1) % groups) for source_idx in range(groups)]
    group_axes = ('pair', 'side')
    head_spec = P(None, None, 'tp', None)
    cache_spec = P(group_axes, None, None, None, 'tp', None)
    prompt_spec = P(group_axes, None, None, 'tp', None)
    row_spec = P(group_axes, None, None)
    spec_in = (row_spec, P(group_axes), row_spec, cache_spec, cache_spec, P(group_axes, None), P(), head_spec, P(), head_spec, head_spec, P(None, 'tp', None, None), P(), P(None, None, 'tp'), P(None, None, 'tp'), P(None, 'tp', None))
    spec_out = (row_spec, row_spec, prompt_spec, prompt_spec, cache_spec, cache_spec)

    def device_step(x_prompt, s_len, y_tok, k_cache, v_cache, c_len, attn_gain, w_q, w_dkv, w_uk, w_uv, w_o, mlp_gain, w_gate, w_up, w_down):
        hidden = x_prompt[0]
        tok_state = y_tok[0]
        seq, dm = hidden.shape
        nb = tok_state.shape[0]
        cur_len = c_len[0]
        wq, wdkv, wuk, wuv = w_q[0], w_dkv[0], w_uk[0], w_uv[0]
        nope, rank = wuk.shape[-1], wuk.shape[0]
        key_old, value_old = k_cache[0, 0], v_cache[0, 0]

        rows = jnp.concatenate([hidden, tok_state], axis=0)
        positions = jnp.concatenate([jnp.arange(seq, dtype=jnp.int32), cur_len.astype(jnp.int32)])
        normed = rms_scaled(rows, attn_gain[0])
        latent_pack = make_latent(normed, wdkv, positions, rank)
        received = lax.ppermute(latent_pack[:seq], 'side', shift_pairs)
        query_all = make_query(normed, wq, positions, nope)
        key_all, value_all = expand_latent(latent_pack, wuk, wuv)
        attn_prompt = prompt_attention(query_all[:seq], key_all[:seq], value_all[:seq], s_len[0])

        slot_hit = (jnp.arange(key_old.shape[1])[None, :] == cur_len[:, None])[:, :, None, None]
        key_next = jnp.where(slot_hit, key_all[seq:, None], key_old)
        value_next = jnp.where(slot_hit, value_all[seq:, None], value_old)
        attn_tok = cache_attention(query_all[seq:], key_next, value_next, cur_len)

        hv = w_o.shape[1] * w_o.shape[2]
        attn_tok = jnp.pad(attn_tok.reshape(nb, hv), ((0, 2 * DEC - nb), (0, 0)))
        h_out, tok_out = finish_block(
            n_tp, attn_prompt.reshape(seq, hv), attn_tok, mlp_gain, hidden, stack_tokens(tok_state),
            w_o[0].reshape(hv, dm), w_gate[0], w_up[0], w_down[0])
        key_in, value_in = expand_latent(received, wuk, wuv)
        return (h_out[None], unstack_tokens(tok_out, nb, dm)[None], key_in[None, None], value_in[None, None], key_next[None, None], value_next[None, None])

    return jax.shard_map(device_step, mesh=mesh, in_specs=spec_in, out_specs=spec_out, check_vma=False)
```

time: 1090 us -> 614 us (0.56)
  blocking collectives: 713 us -> 0 us
  Pallas kernels: 0 us -> 378 us
  matrix products: 276 us -> 118 us
  local copies, waits for them, and re-layouts: 17.8 us -> 40.8 us
    psum x2 -> x0, blocking collectives: 713 us -> none  [tp_sum(): return lax.psum(values, 'tp')]
    pallas_call x0 -> x1, Pallas kernels: none -> 378 us  [finish_block(): pl.pallas_call(functools.partial(block_kernel, n_tp), out_shape=(jax.Shap...]
    dot_general x8 -> x0, matrix products: 174 us -> none  [the longest x2 46.5 us: mlp_partial(): return jnp.dot(act_val, w_down_layer, preferred_element_type=jnp.float32)]
    unnamed x3 -> x2, matrix products: 45.6 us -> 61 us
  transfers between devices with their start and end apart: 1 -> 1, of which waited for: 0 -> 0; matrix products, arithmetic and copies ran while one was open for 31% -> 31% of each run, Pallas kernels for 0% -> 62%
where the time goes in v1:
time: 614 us; the launch traced here: 609 us
  Pallas kernels  378 us (62%)
  matrix products  118 us (19%)
  other arithmetic  69.8 us (11%)
  local copies, waits for them, and re-layouts  40.8 us (7%)
    pallas_call x1, Pallas kernels, finish_block(): pl.pallas_call(functools.partial(block_kernel, n_tp), out_shape=(jax.Shap...  378 us
    unnamed x2, matrix products  61 us
    sub x1, other arithmetic, masked_softmax(): jax.nn.softmax(jnp.where(allowed, scores, -1e+30), axis=-1)  34.4 us
    dot_general x1, matrix products, prompt_attention(): jnp.einsum('qhe,khe->hqk', query_all, key_full, preferred_element_type=jn...  17.1 us
    unnamed x41, local copies, waits for them, and re-layouts  16.5 us
    dot_general x1, matrix products, prompt_attention(): jnp.einsum('hqk,khv->qhv', probs_bf, value_full, preferred_element_type=j...  15.4 us
  transfers between devices with their start and end apart: 1, of which 0 were waited for; matrix products, arithmetic and copies ran while one was open for 31% of the time, Pallas kernels for 62%

profile of v1, /device:TPU:0, one launch (start us, length us, event | category | flops | bytes accessed | tf_op | source)
XLA Modules:
  0.0 609.0 jit_solution(10679603761992967391)
XLA Ops:
  0.6 0.0 copy-start.11
  0.6 0.0 copy-start.1
  0.7 3.8 fusion.8
  4.5 0.8 mul.146
  5.2 0.0 copy-done.11
  5.2 0.0 copy-done.1
  5.2 0.0 copy-start.14
  5.2 7.7 %fusion.39 = bf16[514,576]{0,1:T(8,128)(2,1)S(1)} fusion(bf16[1,5120,576]{1,2,0:T(8,128)(2,1)} %param.24, f32[5120]{0:T(1024)S(1)} %bitcast.92, f32[514]{0:T(1024)S(1)} %add_rsqrt_fusion.1, bf16[2,5120]{1,0:T(2,128)(2,1)S(1)} %bitcast.88, bf16[512,5120]{1,0:T(8,128)(2,1)S(1)} %bitcast.78), kind=kOutput, calls=%fused_computation.55 | convolution fusion | flops 3050413056 | bytes 11776264 | tf_op jit(solution)/shard_map/dot_general | solution.py:52
  12.9 0.2 fusion.42
  13.1 0.1 fusion.43
  13.2 0.0 copy-done.14
  13.3 0.4 multiply_cosine_fusion
  13.6 0.9 pad_maximum_fusion.2
  14.5 1.0 collective-permute-start
  15.5 0.1 iota_compare_fusion.3
  15.6 57.5 %fusion.74 = f32[514,6144]{0,1} fusion(bf16[5120,6144]{0,1:T(8,128)(2,1)} %bitcast.97, f32[5120]{0:T(1024)S(1)} %bitcast.93, f32[514]{0:T(1024)S(1)} %add_rsqrt_fusion.1, bf16[2,5120]{1,0:T(2,128)(2,1)S(1)} %bitcast.89, bf16[512,5120]{1,0:T(8,128)(2,1)} %bitcast.76), kind=kOutput, calls=%fused_computation.108 | convolution fusion | flops 32356505600 | bytes 80832520
  73.1 9.7 %convert_element_type.89 = bf16[514,32,192]{0,2,1:T(8,128)(2,1)} convert(f32[514,32,192]{0,2,1:T(8,128)} %bitcast.80) | non-fusion elementwise | flops 3158016 | bytes 18948096 | tf_op jit(solution)/shard_map/convert_element_type | solution.py:47
  82.8 2.9 slice.76
  85.7 2.6 fusion.33
  88.3 1.6 maximum_bitcast_fusion.1
  89.9 3.6 pad_maximum_fusion
  94.2 0.1 fusion.49
  94.3 0.1 copy.101
  94.4 7.7 %copy.111 = bf16[512,32,128]{0,2,1:T(8,128)(2,1)} copy(bf16[512,32,128]{2,1,0:T(8,128)(2,1)} %bitcast.82) | data formatting | bytes 8388608 | tf_op jit(solution)/shard_map/squeeze | solution.py:489
  102.2 5.2 convolution_convert_fusion
  107.4 0.0 copy-start.3
  107.4 0.5 broadcast_in_dim.108
  107.9 0.0 copy-start
  107.9 2.3 copy-done
  110.3 0.4 copy-done.3
  110.7 1.8 copy-done.16
  112.5 2.9 fusion.24
  115.4 0.0 copy-start.15
  115.5 2.0 copy-done.15
  117.4 2.6 copy.122
  120.0 0.0 copy-done.4
  120.0 1.5 bitcast_select_fusion.2
  121.6 0.0 copy-done.12
  121.6 0.0 copy-done.9
  121.6 3.5 fusion.22
  125.1 0.2 fusion.48
  125.3 0.8 fusion.36
  126.1 0.7 pad.9.clone
  126.8 0.7 pad.8.ad_ref
  127.5 17.1 %fusion.12 = f32[32,512,512]{1,2,0:T(8,128)} fusion(bf16[514,32,128]{2,0,1:T(8,128)(2,1)} %copy-done.3, bf16[514,32,64]{2,0,1:T(8,128)(2,1)} %copy-done, bf16[514,32,192]{0,2,1:T(8,128)(2,1)} %pad_maximum_fusion), kind=kOutput, calls=%fused_computation.19 | convolution fusion | flops 3233808384 | bytes 48365568 | tf_op jit(solution)/shard_map/qhe,khe->hqk/dot_general | solution.py:72
  144.6 34.4 %fusion.77 = (f32[32,512]{1,0:T(8,128)S(1)}, f32[32,512,512]{1,2,0:T(8,128)}) fusion(f32[32,512,512]{1,2,0:T(8,128)} %fusion.12, pred[512,512]{0,1:T(8,128)(4,1)S(1)} %fusion.49), kind=kOutput, calls=%fused_computation.109 | output fusion | flops 50332160 | bytes 67436544 | tf_op jit(solution)/shard_map/sub | solution.py:67
  179.0 15.4 %fusion.27 = bf16[32,128,512]{2,1,0:T(8,128)(2,1)} fusion(f32[32,512,512]{1,2,0:T(8,128)} %get-tuple-element.51, f32[32,512]{1,0:T(8,128)S(1)} %get-tuple-element.50, bf16[514,32,128]{2,0,1:T(8,128)(2,1)} %copy-done.15), kind=kOutput, calls=%fused_computation.42 | convolution fusion | flops 2166358016 | bytes 42008576 | tf_op jit(solution)/shard_map/hqk,khv->qhv/dot_general | solution.py:77
  194.5 6.3 %copy.129.ap_ref = bf16[512,4096]{1,0:T(8,128)(2,1)} copy(bf16[512,4096]{0,1:T(8,128)(2,1)} %bitcast.83) | data formatting | bytes 8388608 | tf_op jit(solution)/shard_map/reshape | solution.py:510
  200.8 378.0 %shard_map.199 = (bf16[512,5120]{1,0:T(8,128)(2,1)}, bf16[2,2,128,128]{3,2,1,0:T(8,128)(2,1)}) custom-call(bf16[512,4096]{1,0:T(8,128)(2,1)} %copy.129.ap_ref, bf16[16,4096]{1,0:T(8,128)(2,1)} %pad.8.ad_ref, bf16[1,5120]{1,0:T(2,128)(2,1)} %gain_ref.1, bf16[512,5120]{1,0:T(8,128)(2,1)} %bitcast.77, bf16[2,2,128,128]{3,2,1,0:T(8,128)(2,1)} %bitcast.84, ...), custom_call_target="tpu_custom_call" | custom-call | tf_op jit(solution)/shard_map/pallas_call | solution.py:435
  578.8 0.0 copy-start.5
  578.8 1.1 slice.81
  579.9 0.6 broadcast_in_dim_reshape.3
  580.5 0.0 copy-done.8
  580.6 2.9 broadcast_select_fusion.1
  583.5 3.2 broadcast_select_fusion
  586.7 0.0 collective-permute-done
  586.7 3.9 convert_bitcast_fusion
  590.6 4.7 copy.115
  595.3 3.5 fusion.53
  598.8 0.6 convert_element_type.101
  599.5 0.8 slice.83
  600.3 0.2 broadcast_in_dim.117
  600.5 3.1 maximum_bitcast_fusion
  603.7 5.2 copy.152
  (34 shorter events, 0.2 us)
Async XLA Ops:
  0.6 4.6 copy-start.11
  0.6 4.6 copy-start.1
  5.2 8.0 %copy-start.14 = (s32[1,2]{1,0:T(1,128)S(1)}, s32[1,2]{1,0:T(1,128)}, u32[]{:S(2)}) copy-start(s32[1,2]{1,0:T(1,128)} %param.21) | copy-start | bytes 28
  14.5 572.1 %collective-permute-start = (bf16[512,576]{0,1:T(8,128)(2,1)}, bf16[512,576]{0,1:T(8,128)(2,1)}, u32[]{:S(2)}, u32[]{:S(2)}) collective-permute-start(bf16[512,576]{0,1:T(8,128)(2,1)} %pad_maximum_fusion.2), channel_id=1, source_target_pairs={{0,1},{1,2},{2,3},{3,0},{4,5},{5,6},{6,7},{7,4},{8,9},{9,10},{10,1... | collective-permute-start | bytes 1769480 | tf_op jit(solution)/shard_map/ppermute | solution.py:497
  15.6 106.0 %copy-start.12 = (pred[2,128]{1,0:T(4,128)(4,1)}, pred[2,128]{1,0:T(4,128)(4,1)S(1)}, u32[]{:S(2)}) copy-start(pred[2,128]{1,0:T(4,128)(4,1)S(1)} %get-tuple-element.49) | copy-start | bytes 772
  107.4 3.3 copy-start.3
  107.9 2.4 copy-start
  110.3 2.2 copy-start.16
  110.7 10.9 %copy-start.9 = (bf16[2,32,192]{2,1,0:T(8,128)(2,1)}, bf16[2,32,192]{2,1,0:T(8,128)(2,1)S(1)}, u32[]{:S(2)}) copy-start(bf16[2,32,192]{2,1,0:T(8,128)(2,1)S(1)} %copy.106) | copy-start | bytes 73732
  112.5 7.5 %copy-start.4 = (bf16[1,1,2,128,32,128]{5,4,3,2,1,0:T(8,128)(2,1)S(1)}, bf16[1,1,2,128,32,128]{5,4,3,2,1,0:T(8,128)(2,1)}, u32[]{:S(2)}) copy-start(bf16[1,1,2,128,32,128]{5,4,3,2,1,0:T(8,128)(2,1)} %param.20) | copy-start | bytes 6291460
  115.4 2.0 copy-start.15
  117.4 7.7 %copy-start.7 = (bf16[2,32,128]{2,1,0:T(8,128)(2,1)}, bf16[2,32,128]{2,1,0:T(8,128)(2,1)S(1)}, u32[]{:S(2)}) copy-start(bf16[2,32,128]{2,1,0:T(8,128)(2,1)S(1)} %copy.107) | copy-start | bytes 49156
  121.6 3.7 copy-start.6
  200.8 379.8 %copy-start.8 = (bf16[2,32,128]{2,1,0:T(8,128)(2,1)S(1)}, bf16[2,32,128]{2,1,0:T(8,128)(2,1)}, u32[]{:S(2)}) copy-start(bf16[2,32,128]{2,1,0:T(8,128)(2,1)} %copy-done.7) | copy-start | bytes 49156
  200.8 379.8 %copy-start.13 = (pred[2,128]{1,0:T(4,128)(4,1)S(1)}, pred[2,128]{1,0:T(4,128)(4,1)}, u32[]{:S(2)}) copy-start(pred[2,128]{1,0:T(4,128)(4,1)} %copy-done.12) | copy-start | bytes 772
  200.8 382.7 %copy-start.10 = (bf16[2,32,192]{2,1,0:T(8,128)(2,1)S(1)}, bf16[2,32,192]{2,1,0:T(8,128)(2,1)}, u32[]{:S(2)}) copy-start(bf16[2,32,192]{2,1,0:T(8,128)(2,1)} %copy-done.9) | copy-start | bytes 73732
  578.8 4.6 copy-start.5
  580.6 6.1 %copy-start.17 = (bf16[1,512,32,128]{3,2,1,0:T(8,128)(2,1)S(1)}, bf16[1,512,32,128]{3,2,1,0:T(8,128)(2,1)}, u32[]{:S(2)}) copy-start(bf16[1,512,32,128]{3,2,1,0:T(8,128)(2,1)} %param.26) | copy-start | bytes 12582916
  590.6 4.7 copy-start.2

commit v2 on v1

--- a/solution.py
+++ b/solution.py
@@ -16,6 +16,7 @@
 RING_OWN = 16
 RING_LAND = 32
 RING_SEND = 16
+RING_HEAD = 3
 DEC = 8
 MESH = pl.DeviceIdType.MESH
 
@@ -43,50 +44,16 @@
     return jnp.concatenate([first_half * cos_part - second_half * sin_part, second_half * cos_part + first_half * sin_part], axis=-1).astype(jnp.bfloat16)
 
 
-def make_query(normed, w_q_layer, positions, nope_dim):
-    query_all = jnp.einsum('sd,dhe->she', normed, w_q_layer, preferred_element_type=jnp.float32).astype(jnp.bfloat16)
-    return jnp.concatenate([query_all[..., :nope_dim], apply_rope(query_all[..., nope_dim:], positions[:, None])], axis=-1)
-
-
 def make_latent(normed, w_dkv_layer, positions, rank_dim):
     latent_raw = jnp.dot(normed, w_dkv_layer, preferred_element_type=jnp.float32).astype(jnp.bfloat16)
     return jnp.concatenate([rms_plain(latent_raw[:, :rank_dim]), apply_rope(latent_raw[:, rank_dim:], positions)], axis=-1)
 
 
-def expand_latent(latent_pack, w_uk_layer, w_uv_layer):
-    rank_dim = w_uk_layer.shape[0]
-    latent = latent_pack[:, :rank_dim]
-    rope_key = latent_pack[:, rank_dim:]
-    key_nope = jnp.einsum('sr,rhn->shn', latent, w_uk_layer, preferred_element_type=jnp.float32).astype(jnp.bfloat16)
-    value_full = jnp.einsum('sr,rhv->shv', latent, w_uv_layer, preferred_element_type=jnp.float32).astype(jnp.bfloat16)
-    rope_heads = jnp.broadcast_to(rope_key[:, None, :], (key_nope.shape[0], key_nope.shape[1], rope_key.shape[1]))
-    return jnp.concatenate([key_nope, rope_heads], axis=-1), value_full
-
-
-def masked_softmax(scores, allowed):
-    return jax.nn.softmax(jnp.where(allowed, scores, -1e30), axis=-1).astype(jnp.bfloat16)
-
-
-def prompt_attention(query_all, key_full, value_full, valid_len):
-    seq_len = query_all.shape[0]
-    scores = jnp.einsum('qhe,khe->hqk', query_all, key_full, preferred_element_type=jnp.float32) * query_all.shape[-1] ** -0.5
-    row_pos = jnp.arange(seq_len)[:, None]
-    col_pos = jnp.arange(seq_len)[None, :]
-    allowed = (col_pos <= row_pos) & (col_pos < valid_len)
-    probs_bf = masked_softmax(scores, allowed[None])
-    return jnp.einsum('hqk,khv->qhv', probs_bf, value_full, preferred_element_type=jnp.float32).astype(jnp.bfloat16)
-
-
-def cache_attention(query_all, key_layer, value_layer, cur_len):
-    scores = jnp.einsum('bhe,bthe->bht', query_all, key_layer, preferred_element_type=jnp.float32) * query_all.shape[-1] ** -0.5
-    allowed = jnp.arange(key_layer.shape[1])[None, None, :] <= cur_len[:, None, None]
-    probs_bf = masked_softmax(scores, allowed)
-    return jnp.einsum('bht,bthv->bhv', probs_bf, value_layer, preferred_element_type=jnp.float32).astype(jnp.bfloat16)
-
-
-def block_kernel(n_tp, ap_ref, ad_ref, gain_ref, x_hbm, ys_hbm, wo_hbm, wg_hbm, wu_hbm, wd_hbm, out_hbm, outd_hbm,
-                 hb, own, land, dec, wa, wb, b_buf, act, stat,
-                 wa_sem, wb_sem, x_sem, out_sem, outd_sem, rs_send, rs_recv, ag_send, ag_recv):
+def block_kernel(n_tp, n_heads, scale, len_ref, clen_ref, kr_ref, cos_ref, sin_ref, rot_ref, gain_ref, a_ref,
+                 wq_hbm, kn_hbm, v_hbm, kt_hbm, vt_hbm,
+                 x_hbm, ys_hbm, wo_hbm, wg_hbm, wu_hbm, wd_hbm, out_hbm, outd_hbm,
+                 hb, own, land, dec, wa, wb, b_buf, act, stat, attn, mask, wq_buf, kn_buf, v_buf, kt_buf, vt_buf,
+                 wa_sem, wb_sem, x_sem, out_sem, outd_sem, rs_send, rs_recv, ag_send, ag_recv, att_sem):
     last = n_tp - 1
     hv = wo_hbm.shape[0]
     dm = wo_hbm.shape[1]
@@ -144,6 +111,70 @@
             pltpu.make_async_copy(wg_hbm.at[:, cols], wb.at[slot, :, pl.ds(0, SUB)], wb_sem.at[slot]).start()
             pltpu.make_async_copy(wu_hbm.at[:, cols], wb.at[slot, :, pl.ds(SUB, SUB)], wb_sem.at[slot]).start()
 
+    nope = kn_hbm.shape[-1]
+    nb = kt_hbm.shape[0]
+    tok_rows = slice(2 * CHUNK, 2 * CHUNK + 2 * DEC)
+
+    def att_copies(g, chunk):
+        slot = g % RING_HEAD
+        keys = pl.ds(0, CHUNK * (chunk + 1))
+        copies = [pltpu.make_async_copy(wq_hbm.at[g], wq_buf.at[slot], att_sem.at[0, slot]),
+                  pltpu.make_async_copy(kn_hbm.at[g, keys], kn_buf.at[slot, keys], att_sem.at[1, slot]),
+                  pltpu.make_async_copy(v_hbm.at[g, keys], v_buf.at[slot, keys], att_sem.at[2, slot])]
+        if chunk == 0:
+            for n in range(nb):
+                copies.append(pltpu.make_async_copy(kt_hbm.at[n, g], kt_buf.at[slot, n], att_sem.at[3 + n, slot]))
+                copies.append(pltpu.make_async_copy(vt_hbm.at[n, g], vt_buf.at[slot, n], att_sem.at[3 + nb + n, slot]))
+        return copies
+
+    def start_att(g, chunk):
+        for copy in att_copies(g, chunk):
+            copy.start()
+
+    def take_rows(ref, chunk):
+        if chunk == 0:
+            return jnp.concatenate([ref[0:CHUNK, :], ref[tok_rows, :]], axis=0)
+        return ref[CHUNK:2 * CHUNK, :]
+
+    def softmax(scores):
+        expd = jnp.exp(scores - jnp.max(scores, axis=-1, keepdims=True))
+        return (expd * (1.0 / jnp.sum(expd, axis=-1, keepdims=True))).astype(jnp.bfloat16)
+
+    def att_step(g, chunk):
+        @pl.when(g + RING_HEAD - 1 < n_heads)
+        def _():
+            start_att(g + RING_HEAD - 1, chunk)
+        for copy in att_copies(g, chunk):
+            copy.wait()
+        slot = g % RING_HEAD
+        keys = CHUNK * (chunk + 1)
+        rows = slice(chunk * CHUNK, (chunk + 1) * CHUNK)
+        cols = pl.ds(pl.multiple_of(g * SUB, SUB), SUB)
+        contract = (((1,), (1,)), ((), ()))
+        f32, bf = jnp.float32, jnp.bfloat16
+        query = lax.dot_general(take_rows(a_ref, chunk), wq_buf[slot], contract, preferred_element_type=f32).astype(bf)
+        flat, raw = query[:, :nope], query[:, nope:]
+        turned = jnp.dot(raw, rot_ref[...], preferred_element_type=f32)
+        rope = (raw.astype(f32) * take_rows(cos_ref, chunk) + turned * take_rows(sin_ref, chunk)).astype(bf)
+        scores = lax.dot_general(flat[:CHUNK], kn_buf[slot, 0:keys, :], contract, preferred_element_type=f32)
+        scores = scores + lax.dot_general(rope[:CHUNK], kr_ref[0:keys, :], contract, preferred_element_type=f32)
+        probs = softmax(jnp.where(mask[rows, 0:keys] > 0, scores * scale, -1e30))
+        attn[rows, cols] = jnp.dot(probs, v_buf[slot, 0:keys, :], preferred_element_type=f32).astype(bf)
+        if chunk == 0:
+            total_tok = jnp.zeros((2 * DEC, SUB), f32)
+            for n in range(nb):
+                kt = kt_buf[slot, n]
+                scores = jnp.dot(flat[CHUNK:], kt[:nope], preferred_element_type=f32)
+                scores = (scores + jnp.dot(rope[CHUNK:], kt[nope:], preferred_element_type=f32)) * scale
+                slots = lax.broadcasted_iota(jnp.int32, scores.shape, 1)
+                probs = softmax(jnp.where(slots <= clen_ref[n:n + 1, :], scores, -1e30))
+                value = jnp.dot(probs, vt_buf[slot, n], preferred_element_type=f32)
+                row = lax.broadcasted_iota(jnp.int32, value.shape, 0)
+                total_tok = jnp.where(row == n, value, total_tok)
+            attn[tok_rows, cols] = total_tok.astype(bf)
+
+    for g in range(RING_HEAD - 1):
+        start_att(g, 0)
     start_a(0)
     start_a(1)
     start_b(0)
@@ -166,6 +197,17 @@
                 pltpu.make_async_copy(ys_hbm.at[d, s], hb.at[d, 4 * nt + s], x_sem).start()
 
     dec[...] = jnp.zeros_like(dec)
+    row_pos = lax.broadcasted_iota(jnp.int32, mask.shape, 0)
+    col_pos = lax.broadcasted_iota(jnp.int32, mask.shape, 1)
+    mask[...] = jnp.where((col_pos <= row_pos) & (col_pos < len_ref[...]), 1.0, 0.0)
+
+    @pl.loop(0, n_heads // 2)
+    def _(g):
+        att_step(2 * g, 0)
+        att_step(2 * g + 1, 0)
+
+    for g in range(RING_HEAD - 1):
+        start_att(g, 1)
 
     pl.semaphore_wait(barrier, jnp.where(z > 0, 1, 0) + jnp.where(z < last, 1, 0))
 
@@ -264,10 +306,7 @@
         start_a(q + 2)
         slot = q % 3
         pltpu.make_async_copy(wa.at[slot, pl.ds(0, hv)], wa.at[slot, pl.ds(0, hv)], wa_sem.at[slot]).wait()
-        if chunk == 0:
-            lhs = ap_ref[0:CHUNK, :]
-        else:
-            lhs = jnp.concatenate([ap_ref[CHUNK:2 * CHUNK, :], ad_ref[...]], axis=0)
+        lhs = attn[0:CHUNK, :] if chunk == 0 else attn[CHUNK:2 * CHUNK + 2 * DEC, :]
         res = jnp.dot(lhs, wa[slot, 0:hv, :], preferred_element_type=jnp.float32)
         store_own(i, q, res, chunk == 1)
 
@@ -334,7 +373,15 @@
     wait_units = (2 * nt - 1 + 2 * last * LAG) // 2 + 1
     wait_all = (4 * nt + 1 + 2 * last * LAG) // 2 + 1
 
-    @pl.loop(0, nt)
+    @pl.loop(0, n_heads // 2)
+    def _(i):
+        wo_step(i, i, 0)
+        tick(2 * i)
+        att_step(2 * i, 1)
+        tick(2 * i + 1)
+        att_step(2 * i + 1, 1)
+
+    @pl.loop(n_heads // 2, nt)
     def _(i):
         wo_step(i, i, 0)
         tick(2 * i)
@@ -422,10 +469,14 @@
     pltpu.make_async_copy(hb.at[:, pl.ds(0, 2)], hb.at[:, pl.ds(0, 2)], outd_sem).wait()
 
 
-def finish_block(n_tp, attn_prompt, attn_tok, mlp_gain, x_rows, y_stack, w_o, w_gate, w_up, w_down):
-    dm = x_rows.shape[1]
+def finish_block(n_tp, scale, len_row, tok_len, rope_key, cos_tab, sin_tab, rot_mat, mlp_gain, normed, w_q, k_nope, value, k_tok, v_tok,
+                 x_rows, y_stack, w_o, w_gate, w_up, w_down):
+    seq, dm = x_rows.shape
     hv = w_o.shape[0]
     ffn = w_gate.shape[1]
+    n_heads, _, nope = k_nope.shape
+    vdim = value.shape[-1]
+    nb, _, qk_dim, slots = k_tok.shape
     nt = dm // 2 // SUB
     units = 2 * (2 * nt + 1)
     bf, f32 = jnp.bfloat16, jnp.float32
@@ -433,9 +484,9 @@
     hbm = pl.BlockSpec(memory_space=pl.ANY)
     sem = pltpu.SemaphoreType.DMA
     return pl.pallas_call(
-        functools.partial(block_kernel, n_tp),
+        functools.partial(block_kernel, n_tp, n_heads, scale),
         out_shape=(jax.ShapeDtypeStruct(x_rows.shape, bf), jax.ShapeDtypeStruct((2, 2, SUB, SUB), bf)),
-        in_specs=[vmem, vmem, vmem, hbm, hbm, hbm, hbm, hbm, hbm],
+        in_specs=[vmem] * 8 + [hbm] * 11,
         out_specs=(hbm, hbm),
         scratch_shapes=[
             pltpu.VMEM((2, 2 * units, SUB, SUB), bf),
@@ -447,11 +498,35 @@
             pltpu.VMEM((CHUNK + 2 * DEC, dm), bf),
             pltpu.VMEM((2, CHUNK + 2 * DEC, ffn), bf),
             pltpu.VMEM((SUB, SUB), f32),
+            pltpu.VMEM((seq + 2 * DEC, hv), bf),
+            pltpu.VMEM((seq, seq), f32),
+            pltpu.VMEM((RING_HEAD, qk_dim, dm), bf),
+            pltpu.VMEM((RING_HEAD, seq, nope), bf),
+            pltpu.VMEM((RING_HEAD, seq, vdim), bf),
+            pltpu.VMEM((RING_HEAD, nb, qk_dim, slots), bf),
+            pltpu.VMEM((RING_HEAD, nb, slots, vdim), bf),
             sem((3,)), sem((3,)), sem, sem, sem,
-            sem((2, RING_OWN)), sem((2, RING_LAND)), sem((2, RING_SEND)), sem((2, RING_LAND)),
+            sem((2, RING_OWN)), sem((2, RING_LAND)), sem((2, RING_SEND)), sem((2, RING_LAND)), sem((3 + 2 * nb, RING_HEAD)),
         ],
         compiler_params=pltpu.CompilerParams(collective_id=0, has_side_effects=True, vmem_limit_bytes=64000 * 1024),
-    )(attn_prompt, attn_tok, mlp_gain, x_rows, y_stack, w_o, w_gate, w_up, w_down)
+    )(len_row, tok_len, rope_key, cos_tab, sin_tab, rot_mat, mlp_gain, normed, w_q, k_nope, value, k_tok, v_tok, x_rows, y_stack, w_o, w_gate, w_up, w_down)
+
+
+def rope_tables(positions, dim):
+    half_dim = dim // 2
+    inv_freq = THETA ** (-jnp.arange(half_dim, dtype=jnp.float32) * 2.0 / dim)
+    angles = positions.astype(jnp.float32)[..., None] * inv_freq
+    cos_part = jnp.cos(angles)
+    sin_part = jnp.sin(angles)
+    return jnp.concatenate([cos_part, cos_part], axis=-1), jnp.concatenate([sin_part, sin_part], axis=-1)
+
+
+def rope_turn(dim):
+    half_dim = dim // 2
+    src = jnp.arange(dim)[:, None]
+    dst = jnp.arange(dim)[None, :]
+    turn = jnp.where(src == dst + half_dim, -1.0, 0.0) + jnp.where(dst == src + half_dim, 1.0, 0.0)
+    return turn.astype(jnp.bfloat16)
 
 
 def stack_tokens(rows):
@@ -490,26 +565,42 @@
         nope, rank = wuk.shape[-1], wuk.shape[0]
         key_old, value_old = k_cache[0, 0], v_cache[0, 0]
 
-        rows = jnp.concatenate([hidden, tok_state], axis=0)
-        positions = jnp.concatenate([jnp.arange(seq, dtype=jnp.int32), cur_len.astype(jnp.int32)])
-        normed = rms_scaled(rows, attn_gain[0])
+        rope_dim = wq.shape[-1] - nope
+        pad_rows = 2 * DEC - nb
+        rows = jnp.concatenate([hidden, tok_state, jnp.zeros((pad_rows, dm), hidden.dtype)], axis=0)
+        positions = jnp.concatenate([jnp.arange(seq, dtype=jnp.int32), cur_len.astype(jnp.int32), jnp.zeros((pad_rows,), jnp.int32)])
+        normed = lax.optimization_barrier(rms_scaled(rows, attn_gain[0]))
         latent_pack = make_latent(normed, wdkv, positions, rank)
         received = lax.ppermute(latent_pack[:seq], 'side', shift_pairs)
-        query_all = make_query(normed, wq, positions, nope)
-        key_all, value_all = expand_latent(latent_pack, wuk, wuv)
-        attn_prompt = prompt_attention(query_all[:seq], key_all[:seq], value_all[:seq], s_len[0])
-
+
+        def per_head(form, left, right):
+            return jnp.einsum(form, left, right, preferred_element_type=jnp.float32).astype(jnp.bfloat16)
+
+        k_nope = per_head('sr,rhn->hsn', latent_pack[:, :rank], wuk)
+        value = per_head('sr,rhv->hsv', latent_pack[:, :rank], wuv)
+
+        tok = slice(seq, seq + nb)
+        n_heads = wuk.shape[1]
+        key_tok = jnp.concatenate([k_nope[:, tok], jnp.broadcast_to(latent_pack[None, tok, rank:], (n_heads, nb, rope_dim))], axis=-1)
+        key_tok = jnp.transpose(key_tok, (1, 0, 2))
+        value_tok = jnp.transpose(value[:, tok], (1, 0, 2))
         slot_hit = (jnp.arange(key_old.shape[1])[None, :] == cur_len[:, None])[:, :, None, None]
-        key_next = jnp.where(slot_hit, key_all[seq:, None], key_old)
-        value_next = jnp.where(slot_hit, value_all[seq:, None], value_old)
-        attn_tok = cache_attention(query_all[seq:], key_next, value_next, cur_len)
+        key_next = jnp.where(slot_hit, key_tok[:, None], key_old)
+        value_next = jnp.where(slot_hit, value_tok[:, None], value_old)
 
         hv = w_o.shape[1] * w_o.shape[2]
-        attn_tok = jnp.pad(attn_tok.reshape(nb, hv), ((0, 2 * DEC - nb), (0, 0)))
+        cos_tab, sin_tab = rope_tables(positions, rope_dim)
+        len_row = jnp.broadcast_to(s_len.astype(jnp.int32)[:, None], (1, seq))
+        tok_len = jnp.broadcast_to(cur_len.astype(jnp.int32)[:, None], (nb, key_old.shape[1]))
         h_out, tok_out = finish_block(
-            n_tp, attn_prompt.reshape(seq, hv), attn_tok, mlp_gain, hidden, stack_tokens(tok_state),
-            w_o[0].reshape(hv, dm), w_gate[0], w_up[0], w_down[0])
-        key_in, value_in = expand_latent(received, wuk, wuv)
+            n_tp, wq.shape[-1] ** -0.5, len_row, tok_len, latent_pack[:seq, rank:], cos_tab, sin_tab, rope_turn(rope_dim), mlp_gain,
+            normed, jnp.transpose(wq, (1, 2, 0)), k_nope, value, jnp.transpose(key_next, (0, 2, 3, 1)), jnp.transpose(value_next, (0, 2, 1, 3)),
+            hidden, stack_tokens(tok_state), w_o[0].reshape(hv, dm), w_gate[0], w_up[0], w_down[0])
+
+        key_in = per_head('sr,rhn->hns', received[:, :rank], wuk)
+        rope_in = jnp.broadcast_to(received[:, rank:].T[None], (n_heads, rope_dim, seq))
+        key_in = jnp.transpose(jnp.concatenate([key_in, rope_in], axis=1), (2, 0, 1))
+        value_in = per_head('sr,rhv->shv', received[:, :rank], wuv)
         return (h_out[None], unstack_tokens(tok_out, nb, dm)[None], key_in[None, None], value_in[None, None], key_next[None, None], value_next[None, None])
 
     return jax.shard_map(device_step, mesh=mesh, in_specs=spec_in, out_specs=spec_out, check_vma=False)

time: 614 us -> 580 us (0.945)
  Pallas kernels: 378 us -> 496 us
  matrix products: 118 us -> 19.4 us
  other arithmetic: 69.8 us -> 30.1 us
  local copies, waits for them, and re-layouts: 40.8 us -> 24.9 us
    pallas_call x1, Pallas kernels: 378 us -> 496 us  [finish_block(): pl.pallas_call(functools.partial(block_kernel, n_tp, n_heads, scale), out...]
    unnamed x2 -> x1, matrix products: 61 us -> 3.38 us
    dot_general x7 -> x3, matrix products: 48.9 us -> 11.6 us  [per_head(): jnp.einsum(form, left, right, preferred_element_type=jnp.float32)]
    sub x1 -> x0, other arithmetic: 34.4 us -> none  [masked_softmax(): jax.nn.softmax(jnp.where(allowed, scores, -1e+30), axis=-1)]
    reshape x1 -> x0, local copies, waits for them, and re-layouts: 6.32 us -> none  [device_step(): attn_prompt.reshape(seq, hv)]
    unnamed x41 -> x32, local copies, waits for them, and re-layouts: 16.5 us -> 11.5 us
  transfers between devices with their start and end apart: 1 -> 1, of which waited for: 0 -> 0; matrix products, arithmetic and copies ran while one was open for 31% -> 6% of each run, Pallas kernels for 62% -> 86%
where the time goes in v2:
time: 580 us; the launch traced here: 573 us
  Pallas kernels  496 us (86%)
  other arithmetic  30.1 us (5%)
  local copies, waits for them, and re-layouts  24.9 us (4%)
  matrix products  19.4 us (3%)
    pallas_call x1, Pallas kernels, finish_block(): pl.pallas_call(functools.partial(block_kernel, n_tp, n_heads, scale), out...  496 us
  transfers between devices with their start and end apart: 1, of which 0 were waited for; matrix products, arithmetic and copies ran while one was open for 6% of the time, Pallas kernels for 86%

profile of v2, /device:TPU:0, one launch (start us, length us, event | category | flops | bytes accessed | tf_op | source)
XLA Modules:
  0.0 573.5 jit_solution(15308729892182270284)
XLA Ops:
  0.6 0.0 copy-start.8
  0.6 0.0 copy-start
  0.7 0.9 mul.87
  1.6 0.1 pad.23.clone
  1.7 4.6 fusion
  6.2 0.0 copy-done.8
  6.2 0.0 copy-done
  6.3 0.0 slice-start.1
  6.3 4.8 fusion.2.a_ref
  11.1 0.0 slice-done
  11.1 0.0 slice-done.1
  11.1 0.0 copy-start.1
  11.2 0.0 copy-start.9
  11.2 4.5 fusion.15
  15.6 0.0 copy-done.1
  15.7 0.2 fusion.18
  15.9 0.2 fusion.19
  16.1 0.0 copy-done.9
  16.1 0.1 add_convert_fusion.1
  16.2 1.1 fusion.29
  17.3 0.1 pad_maximum_fusion
  17.4 1.1 copy.69
  18.5 1.0 collective-permute-start
  19.5 0.8 fusion.30.kr_ref
  20.3 0.1 iota_compare_fusion.2
  20.3 0.1 pad_maximum_fusion.4
  21.1 0.7 add_convert_fusion.rot_ref
  21.8 7.5 %copy.71 = bf16[512,32,128]{0,2,1:T(8,128)(2,1)} copy(bf16[512,32,128]{2,1,0:T(8,128)(2,1)} %bitcast.82) | data formatting | bytes 8388608 | tf_op jit(solution)/shard_map/squeeze | solution.py:564
  29.2 5.0 convert_bitcast_fusion.1.kn_hbm
  34.3 0.0 copy-start.6
  34.3 0.0 copy-done.10
  34.3 0.0 copy-start.3
  34.3 2.6 convert_bitcast_fusion.v_hbm
  36.9 0.0 copy-done.6
  37.0 0.0 copy-start.7
  37.0 0.0 copy-start.5
  37.1 0.7 pad.4.clone
  37.8 1.0 pad_maximum_fusion.2
  38.8 0.0 copy-done.3
  38.8 3.2 fusion.9.kt_hbm
  42.0 0.0 copy-done.5
  42.0 2.2 fusion.14.vt_hbm
  44.2 0.0 copy-done.7
  44.2 0.6 broadcast_in_dim.107.len_ref
  44.8 0.6 broadcast_in_dim.109.clen_ref
  45.4 496.0 %shard_map.199 = (bf16[512,5120]{1,0:T(8,128)(2,1)}, bf16[2,2,128,128]{3,2,1,0:T(8,128)(2,1)}) custom-call(s32[1,512]{1,0:T(1,128)} %broadcast_in_dim.107.len_ref, s32[2,128]{1,0:T(2,128)} %broadcast_in_dim.109.clen_ref, bf16[512,64]{1,0:T(8,128)(2,1)} %fusion.30.kr_ref, f32[528,64]{1,0:T(8,128)} %get-tuple-element.38.cos_ref, ...), custom_call_target="tpu_custom_call" | custom-call | tf_op jit(solution)/shard_map/pallas_call | solution.py:486
  541.4 0.0 copy-start.4
  541.4 1.1 slice.55
  542.5 0.6 broadcast_in_dim_reshape.3
  543.1 3.1 broadcast_select_fusion.1
  546.3 0.0 copy-done.4
  546.3 3.2 broadcast_select_fusion
  549.4 0.0 collective-permute-done
  549.4 0.0 copy-done.2
  549.5 3.4 fusion.23
  552.8 0.0 copy-start.11
  552.8 0.6 convert_bitcast_fusion.3
  553.5 1.5 copy-done.11
  555.0 3.9 convert_bitcast_fusion.2
  559.0 4.7 copy.75
  563.7 0.8 slice_bitcast_fusion
  564.5 0.2 broadcast_in_dim.120
  564.8 3.1 maximum_bitcast_fusion
  567.9 5.2 copy.92
  (20 shorter events, 0.2 us)
Async XLA Ops:
  0.6 5.6 copy-start.8
  0.6 5.6 copy-start
  1.7 9.5 %slice-start = ((s8[5898240]{0:T(1024)(128)(4,1)}), s8[4194304]{0:T(1024)(128)(4,1)S(1)}, s32[]{:S(2)}) async-start(s8[5898240]{0:T(1024)(128)(4,1)} %bitcast.93), calls=%async_computation | async-start | bytes 8388608
  6.3 4.9 slice-start.1
  11.1 4.5 copy-start.1
  11.2 4.9 copy-start.9
  18.5 531.0 %collective-permute-start = (bf16[512,576]{0,1:T(8,128)(2,1)}, bf16[512,576]{0,1:T(8,128)(2,1)}, u32[]{:S(2)}, u32[]{:S(2)}) collective-permute-start(bf16[512,576]{0,1:T(8,128)(2,1)} %copy.69), channel_id=1, source_target_pairs={{0,1},{1,2},{2,3},{3,0},{4,5},{5,6},{6,7},{7,4},{8,9},{9,10},{10,1... | collective-permute-start | bytes 1769480 | tf_op jit(solution)/shard_map/ppermute | solution.py:574
  29.2 5.0 copy-start.10
  34.3 2.7 copy-start.6
  34.3 4.5 copy-start.3
  37.0 7.2 %copy-start.7 = (bf16[32,528,128]{2,1,0:T(8,128)(2,1)}, bf16[32,528,128]{2,1,0:T(8,128)(2,1)S(1)}, u32[]{:S(2)}) copy-start(bf16[32,528,128]{2,1,0:T(8,128)(2,1)S(1)} %convert_bitcast_fusion.v_hbm) | copy-start | bytes 12976132
  37.0 5.0 copy-start.5
  541.4 4.8 copy-start.4
  543.1 6.3 %copy-start.2 = (bf16[512,32,128]{0,2,1:T(8,128)(2,1)S(1)}, bf16[512,32,128]{0,2,1:T(8,128)(2,1)}, u32[]{:S(2)}) copy-start(bf16[512,32,128]{0,2,1:T(8,128)(2,1)} %copy.71) | copy-start | bytes 12582916
  552.8 2.2 copy-start.11

commit v3 on v2

--- a/solution.py
+++ b/solution.py
@@ -16,7 +16,7 @@
 RING_OWN = 16
 RING_LAND = 32
 RING_SEND = 16
-RING_HEAD = 3
+RING_HEAD = 4
 DEC = 8
 MESH = pl.DeviceIdType.MESH
 
@@ -140,22 +140,34 @@
         expd = jnp.exp(scores - jnp.max(scores, axis=-1, keepdims=True))
         return (expd * (1.0 / jnp.sum(expd, axis=-1, keepdims=True))).astype(jnp.bfloat16)
 
-    def att_step(g, chunk):
-        @pl.when(g + RING_HEAD - 1 < n_heads)
-        def _():
-            start_att(g + RING_HEAD - 1, chunk)
-        for copy in att_copies(g, chunk):
-            copy.wait()
+    def att_pair(g, chunk):
+        @pl.when(g + 2 < n_heads)
+        def _():
+            start_att(g + 2, chunk)
+            start_att(g + 3, chunk)
+        for k in (0, 1):
+            for copy in att_copies(g + k, chunk):
+                copy.wait()
+        queries = [project(g + k, chunk) for k in (0, 1)]
+        for k in (0, 1):
+            attend(g + k, chunk, *queries[k])
+
+    def project(g, chunk):
+        contract = (((1,), (1,)), ((), ()))
+        f32, bf = jnp.float32, jnp.bfloat16
+        query = lax.dot_general(take_rows(a_ref, chunk), wq_buf[g % RING_HEAD], contract, preferred_element_type=f32).astype(bf)
+        flat, raw = query[:, :nope], query[:, nope:]
+        turned = jnp.dot(raw, rot_ref[...], preferred_element_type=f32)
+        rope = (raw.astype(f32) * take_rows(cos_ref, chunk) + turned * take_rows(sin_ref, chunk)).astype(bf)
+        return flat, rope
+
+    def attend(g, chunk, flat, rope):
         slot = g % RING_HEAD
         keys = CHUNK * (chunk + 1)
         rows = slice(chunk * CHUNK, (chunk + 1) * CHUNK)
         cols = pl.ds(pl.multiple_of(g * SUB, SUB), SUB)
         contract = (((1,), (1,)), ((), ()))
         f32, bf = jnp.float32, jnp.bfloat16
-        query = lax.dot_general(take_rows(a_ref, chunk), wq_buf[slot], contract, preferred_element_type=f32).astype(bf)
-        flat, raw = query[:, :nope], query[:, nope:]
-        turned = jnp.dot(raw, rot_ref[...], preferred_element_type=f32)
-        rope = (raw.astype(f32) * take_rows(cos_ref, chunk) + turned * take_rows(sin_ref, chunk)).astype(bf)
         scores = lax.dot_general(flat[:CHUNK], kn_buf[slot, 0:keys, :], contract, preferred_element_type=f32)
         scores = scores + lax.dot_general(rope[:CHUNK], kr_ref[0:keys, :], contract, preferred_element_type=f32)
         probs = softmax(jnp.where(mask[rows, 0:keys] > 0, scores * scale, -1e30))
@@ -173,7 +185,7 @@
                 total_tok = jnp.where(row == n, value, total_tok)
             attn[tok_rows, cols] = total_tok.astype(bf)
 
-    for g in range(RING_HEAD - 1):
+    for g in (0, 1):
         start_att(g, 0)
     start_a(0)
     start_a(1)
@@ -203,10 +215,9 @@
 
     @pl.loop(0, n_heads // 2)
     def _(g):
-        att_step(2 * g, 0)
-        att_step(2 * g + 1, 0)
-
-    for g in range(RING_HEAD - 1):
+        att_pair(2 * g, 0)
+
+    for g in (0, 1):
         start_att(g, 1)
 
     pl.semaphore_wait(barrier, jnp.where(z > 0, 1, 0) + jnp.where(z < last, 1, 0))
@@ -377,9 +388,8 @@
     def _(i):
         wo_step(i, i, 0)
         tick(2 * i)
-        att_step(2 * i, 1)
-        tick(2 * i + 1)
-        att_step(2 * i + 1, 1)
+        att_pair(2 * i, 1)
+        tick(2 * i + 1)
 
     @pl.loop(n_heads // 2, nt)
     def _(i):
@@ -585,7 +595,7 @@
         key_tok = jnp.transpose(key_tok, (1, 0, 2))
         value_tok = jnp.transpose(value[:, tok], (1, 0, 2))
         slot_hit = (jnp.arange(key_old.shape[1])[None, :] == cur_len[:, None])[:, :, None, None]
-        key_next = jnp.where(slot_hit, key_tok[:, None], key_old)
+        key_next = lax.optimization_barrier(jnp.transpose(jnp.where(slot_hit, key_tok[:, None], key_old), (0, 2, 3, 1)))
         value_next = jnp.where(slot_hit, value_tok[:, None], value_old)
 
         hv = w_o.shape[1] * w_o.shape[2]
@@ -594,13 +604,13 @@
         tok_len = jnp.broadcast_to(cur_len.astype(jnp.int32)[:, None], (nb, key_old.shape[1]))
         h_out, tok_out = finish_block(
             n_tp, wq.shape[-1] ** -0.5, len_row, tok_len, latent_pack[:seq, rank:], cos_tab, sin_tab, rope_turn(rope_dim), mlp_gain,
-            normed, jnp.transpose(wq, (1, 2, 0)), k_nope, value, jnp.transpose(key_next, (0, 2, 3, 1)), jnp.transpose(value_next, (0, 2, 1, 3)),
+            normed, jnp.transpose(wq, (1, 2, 0)), k_nope, value, key_next, jnp.transpose(value_next, (0, 2, 1, 3)),
             hidden, stack_tokens(tok_state), w_o[0].reshape(hv, dm), w_gate[0], w_up[0], w_down[0])
 
         key_in = per_head('sr,rhn->hns', received[:, :rank], wuk)
         rope_in = jnp.broadcast_to(received[:, rank:].T[None], (n_heads, rope_dim, seq))
         key_in = jnp.transpose(jnp.concatenate([key_in, rope_in], axis=1), (2, 0, 1))
         value_in = per_head('sr,rhv->shv', received[:, :rank], wuv)
-        return (h_out[None], unstack_tokens(tok_out, nb, dm)[None], key_in[None, None], value_in[None, None], key_next[None, None], value_next[None, None])
+        return (h_out[None], unstack_tokens(tok_out, nb, dm)[None], key_in[None, None], value_in[None, None], jnp.transpose(key_next, (0, 3, 1, 2))[None, None], value_next[None, None])
 
     return jax.shard_map(device_step, mesh=mesh, in_specs=spec_in, out_specs=spec_out, check_vma=False)

time: 580 us -> 564 us (0.972)
  Pallas kernels: 496 us -> 488 us
    pallas_call x1, Pallas kernels: 496 us -> 488 us  [finish_block(): pl.pallas_call(functools.partial(block_kernel, n_tp, n_heads, scale), out...]
  transfers between devices with their start and end apart: 1 -> 1, of which waited for: 0 -> 0; matrix products, arithmetic and copies ran while one was open for 6% -> 5% of each run, Pallas kernels for 86% -> 87%
where the time goes in v3:
time: 564 us; the launch traced here: 558 us
  Pallas kernels  488 us (87%)
  other arithmetic  26.9 us (5%)
  local copies, waits for them, and re-layouts  23 us (4%)
  matrix products  17.4 us (3%)
    pallas_call x1, Pallas kernels, finish_block(): pl.pallas_call(functools.partial(block_kernel, n_tp, n_heads, scale), out...  488 us
    unnamed x30, local copies, waits for them, and re-layouts  11.5 us
  transfers between devices with their start and end apart: 1, of which 0 were waited for; matrix products, arithmetic and copies ran while one was open for 5% of the time, Pallas kernels for 87%

profile of v3, /device:TPU:0, one launch (start us, length us, event | category | flops | bytes accessed | tf_op | source)
XLA Modules:
  0.0 558.2 jit_solution(10055451059311987281)
XLA Ops:
  0.6 0.0 copy-start.7
  0.6 0.0 copy-start
  0.7 0.9 mul.87
  1.6 0.1 pad.23.clone
  1.7 0.0 slice-start
  1.7 4.6 fusion
  6.2 0.0 copy-done.7
  6.2 0.0 copy-done
  6.3 0.0 slice-start.1
  6.3 4.8 fusion.2.a_ref
  11.1 0.0 slice-done
  11.1 0.0 slice-done.1
  11.1 0.0 copy-start.1
  11.2 0.0 copy-start.8
  11.2 4.5 fusion.15
  15.6 0.0 copy-done.1
  15.7 0.2 fusion.18
  15.9 0.2 fusion.19
  16.1 0.0 copy-done.8
  16.1 0.1 add_convert_fusion.1
  16.2 1.1 fusion.29
  17.3 0.1 pad_maximum_fusion
  17.4 0.2 copy.66
  17.6 1.1 collective-permute-start
  18.7 0.8 fusion.30.kr_ref
  19.5 0.1 iota_compare_fusion.2
  19.6 0.1 pad_maximum_fusion.4
  19.7 7.5 %copy.68 = bf16[512,32,128]{0,2,1:T(8,128)(2,1)} copy(bf16[512,32,128]{2,1,0:T(8,128)(2,1)} %bitcast.86) | data formatting | bytes 8388608 | tf_op jit(solution)/shard_map/squeeze | solution.py:574
  27.1 0.0 copy-start.9
  27.1 5.0 convert_bitcast_fusion.1.kn_hbm
  32.2 0.0 copy-start.4
  32.2 0.0 copy-done.9
  32.2 0.0 copy-start.6
  32.2 2.6 convert_bitcast_fusion.v_hbm
  34.8 0.0 copy-done.4
  34.8 0.0 copy-start.5
  34.9 0.0 copy-start.3
  35.0 1.0 pad_maximum_fusion.2
  36.0 0.0 copy-done.6
  36.0 3.2 fusion.9.kt_hbm
  39.2 0.0 copy-done.3
  39.2 2.2 fusion.14.vt_hbm
  41.4 0.0 copy-done.5
  42.1 0.7 pad.4.clone
  42.8 0.7 add_convert_fusion.rot_ref
  43.4 0.6 broadcast_in_dim.105.len_ref
  44.0 0.6 broadcast_in_dim.107.clen_ref
  44.7 487.7 %shard_map.199 = (bf16[512,5120]{1,0:T(8,128)(2,1)}, bf16[2,2,128,128]{3,2,1,0:T(8,128)(2,1)}) custom-call(s32[1,512]{1,0:T(1,128)} %broadcast_in_dim.105.len_ref, s32[2,128]{1,0:T(2,128)} %broadcast_in_dim.107.clen_ref, bf16[512,64]{1,0:T(8,128)(2,1)} %fusion.30.kr_ref, f32[528,64]{1,0:T(8,128)} %get-tuple-element.38.cos_ref, ...), custom_call_target="tpu_custom_call" | custom-call | tf_op jit(solution)/shard_map/pallas_call | solution.py:496
  532.3 0.9 slice.55
  533.3 0.6 broadcast_in_dim_reshape.3
  533.9 0.0 copy-start.2
  533.9 3.1 broadcast_select_fusion
  537.0 0.0 collective-permute-done
  537.0 0.0 copy-done.2
  537.0 2.3 fusion.23
  539.4 0.0 copy-start.10
  539.4 0.6 convert_bitcast_fusion.3
  540.0 1.5 copy-done.10
  541.6 2.9 convert_bitcast_fusion.2
  544.5 4.7 copy.71
  549.2 0.2 broadcast_in_dim.118
  549.4 3.1 maximum_bitcast_fusion
  552.5 5.2 copy.88
  (18 shorter events, 0.2 us)
Async XLA Ops:
  0.6 5.6 %copy-start.7 = (bf16[1,2,5120]{2,1,0:T(2,128)(2,1)S(1)}, bf16[1,2,5120]{2,1,0:T(2,128)(2,1)}, u32[]{:S(2)}) copy-start(bf16[1,2,5120]{2,1,0:T(2,128)(2,1)} %param.18) | copy-start | bytes 61444
  0.6 5.6 %copy-start = (bf16[1,512,5120]{2,1,0:T(8,128)(2,1)S(1)}, bf16[1,512,5120]{2,1,0:T(8,128)(2,1)}, u32[]{:S(2)}) copy-start(bf16[1,512,5120]{2,1,0:T(8,128)(2,1)} %param.16) | copy-start | bytes 15728644
  1.7 9.5 %slice-start = ((s8[5898240]{0:T(1024)(128)(4,1)}), s8[4194304]{0:T(1024)(128)(4,1)S(1)}, s32[]{:S(2)}) async-start(s8[5898240]{0:T(1024)(128)(4,1)} %bitcast.97), calls=%async_computation | async-start | bytes 8388608
  6.3 4.9 slice-start.1
  11.1 4.5 copy-start.1
  11.2 4.9 copy-start.8
  17.6 519.4 %collective-permute-start = (bf16[512,576]{0,1:T(8,128)(2,1)S(1)}, bf16[512,576]{0,1:T(8,128)(2,1)S(1)}, u32[]{:S(2)}, u32[]{:S(2)}) collective-permute-start(bf16[512,576]{0,1:T(8,128)(2,1)S(1)} %copy.66), channel_id=1, source_target_pairs={{0,1},{1,2},{2,3},{3,0},{4,5},{5,6},{6,7},{7,4},{8,9},{9,10},{10,1... | collective-permute-start | bytes 1769480 | tf_op jit(solution)/shard_map/ppermute | solution.py:584
  27.1 5.0 copy-start.9
  32.2 2.7 copy-start.4
  32.2 3.8 copy-start.6
  34.8 6.5 %copy-start.5 = (bf16[32,528,128]{2,1,0:T(8,128)(2,1)}, bf16[32,528,128]{2,1,0:T(8,128)(2,1)S(1)}, u32[]{:S(2)}) copy-start(bf16[32,528,128]{2,1,0:T(8,128)(2,1)S(1)} %convert_bitcast_fusion.v_hbm) | copy-start | bytes 12976132
  34.9 4.3 copy-start.3
  533.9 3.1 copy-start.2
  539.4 2.2 copy-start.10
